TPU v7x, 128 devices: a whole 4x4x4 slice. The times are simulated.
128 devices in a mesh: batch: 4 (over y), expert: 8 (over x, core), tensor: 4 (over z).
Axes of the slice: x: 4, y: 4, z: 4, core: 2. Of those that a mesh axis runs over, the one named last changes fastest.
Arguments:
- tokens: bfloat16 [8, 1024, 4096], P('expert', 'batch', 'tensor'), may hold values from -8 to 8
- gain: bfloat16 [4096], P('tensor'), may hold values from 0.5 to 1.5
- phi: bfloat16 [4096, 512], P('tensor'), may hold values from -1 to 1
- w_gate: bfloat16 [8, 4096, 14336], P('expert', None, ('batch', 'tensor')), may hold values from -0.125 to 0.125
- w_up: bfloat16 [8, 4096, 14336], P('expert', None, ('batch', 'tensor')), may hold values from -0.125 to 0.125
- w_down: bfloat16 [8, 14336, 4096], P('expert', ('batch', 'tensor')), may hold values from -0.09375 to 0.09375
Outputs:
- moe_out: bfloat16 [8, 1024, 4096], P('expert', 'batch', 'tensor')
All inputs are finite; a program needn't handle non-finite values.
Results may differ from a plain program's by a relative error of at most 0.025.
Values may be sent and summed in bfloat16 or wider, within the bound.
A program may use at most 128 MiB of HBM per device.

v0:
```python
import jax
import jax.numpy as jnp
from jax import lax
from jax.sharding import PartitionSpec as P

D = 4096
P_SIZE = 64


def sent_to_all(x, axis):
    size = lax.axis_size(axis)
    return lax.all_to_all(jnp.broadcast_to(x[None], (size, *x.shape)), axis, 0, 0, tiled=True)


def of_everyone(x, axis):
    return sent_to_all(x, axis).sum(axis=0)


def packed_total(arrays, axis):
    ends = [0]
    for a in arrays:
        ends.append(ends[-1] + a.size)
    running = of_everyone(jnp.concatenate([a.ravel() for a in arrays]), axis)
    return tuple((running[b:e].reshape(a.shape) for a, b, e in zip(arrays, ends, ends[1:])))


def collected_together(x, axis):
    leaves = jax.tree.leaves(x)
    order = sorted(range(len(leaves)), key=lambda k: -leaves[k].size)
    width = (1, *leaves[order[0]].shape)[-1]
    lines = [
        jnp.pad(leaves[k].reshape(-1), (0, -leaves[k].size % width)).reshape(-1, width)
        for k in order
    ]
    both, at, found = (sent_to_all(jnp.concatenate(lines), axis), 0, {})
    for k, line in zip(order, lines):
        piece = both[:, at : at + len(line)].reshape(len(both), -1)
        found[k] = piece[:, : leaves[k].size].reshape(-1, *leaves[k].shape)
        at += len(line)
    numbers = iter(range(len(leaves)))
    return jax.tree.map(lambda _: found[next(numbers)], x)


def combined_pairwise(pieces, combine):
    while len(jax.tree.leaves(pieces)[0]) > 1:
        pieces = jax.vmap(combine)(
            *(jax.tree.map(lambda part: part[side::2], pieces) for side in (0, 1))
        )
    return jax.tree.map(lambda part: part[0], pieces)


def joined_all(x, axis, combine):
    pieces = collected_together(x, axis)
    return combined_pairwise(pieces, combine)


def cut_along(x, dim, size):
    dims = x.shape
    parts = x.reshape(*dims[:dim], size, dims[dim] // size, *dims[dim + 1 :])
    return jnp.moveaxis(parts, dim, 0)


def summed_on_arrival(x, axis, dim):
    size = lax.axis_size(axis)
    parts = lax.all_to_all(cut_along(x, dim, size), axis, 0, 0, tiled=True)
    return jnp.sum(parts.astype(jnp.float32), axis=0)


def laid_out(parts, dim):
    dims = list(parts.shape[1:])
    dims[dim] *= parts.shape[0]
    return jnp.moveaxis(parts, 0, dim).reshape(dims)


def collect(x, axis, dim):
    parts = sent_to_all(x, axis)
    return laid_out(parts, dim)


def joint_totals(left_pair, right_pair):
    new_max = jnp.maximum(left_pair[0], right_pair[0])
    merged = left_pair[1] * jnp.exp(left_pair[0] - new_max) + right_pair[1] * jnp.exp(
        right_pair[0] - new_max
    )
    return (new_max, merged)


def local(tokens, gain, phi, w_gate, w_up, w_down):
    tokens_f = tokens[0].astype(jnp.float32)
    gain_f = gain.astype(jnp.float32)
    scaled = (tokens_f * gain_f[None, :]).astype(jnp.bfloat16)
    squares = jnp.sum(tokens_f * tokens_f, axis=1)
    partial_logits = jnp.dot(scaled, phi, preferred_element_type=jnp.float32)
    squares, partial_logits = packed_total((squares, partial_logits), "tensor")
    inv_rms = lax.rsqrt(squares / D + 1e-06)
    logits = partial_logits * inv_rms[:, None]
    normed = (tokens_f * gain_f[None, :] * inv_rms[:, None]).astype(jnp.bfloat16)
    combine = jax.nn.softmax(logits, axis=1).astype(jnp.bfloat16)
    local_max = jnp.max(logits, axis=0)
    local_total = jnp.sum(jnp.exp(logits - local_max[None, :]), axis=0)
    column_max, column_total = joined_all((local_max, local_total), "batch", joint_totals)
    dispatch = (jnp.exp(logits - column_max[None, :]) / column_total[None, :]).astype(jnp.bfloat16)
    slot_partial = jnp.einsum("ts,td->sd", dispatch, normed, preferred_element_type=jnp.float32)
    per_device = w_gate.shape[0]
    experts = phi.shape[1] // P_SIZE
    width_share = tokens.shape[2]
    slot_partial = slot_partial.reshape(experts, P_SIZE, width_share)
    quarter = summed_on_arrival(slot_partial.astype(jnp.bfloat16), "batch", 1).astype(jnp.bfloat16)
    exchanged = lax.all_to_all(quarter, "expert", split_axis=0, concat_axis=0, tiled=True)
    arrived = collect(exchanged, "batch", 1)
    groups = arrived.shape[0] // per_device
    arrived = arrived.reshape(groups, per_device, P_SIZE, width_share)
    hidden_share = w_gate.shape[2]
    shard_piece = lax.all_gather(arrived, "tensor", axis=3, tiled=True)
    gate_next = jnp.einsum(
        "gxpd,xdf->gxpf", shard_piece, w_gate, preferred_element_type=jnp.float32
    )
    up_next = jnp.einsum("gxpd,xdf->gxpf", shard_piece, w_up, preferred_element_type=jnp.float32)
    hidden = (jax.nn.silu(gate_next) * up_next).astype(jnp.bfloat16)
    batch_count = lax.axis_size("batch")
    tensor_count = lax.axis_size("tensor")
    hidden = hidden.reshape(groups, per_device, batch_count, P_SIZE // batch_count, hidden_share)
    down_split = w_down.reshape(per_device, hidden_share, tensor_count, D // tensor_count)
    partials = jnp.einsum(
        "gxbqf,xftd->btgxqd", hidden, down_split, preferred_element_type=jnp.float32
    )
    partials = partials.reshape(
        batch_count * tensor_count, groups, per_device, P_SIZE // batch_count, width_share
    ).astype(jnp.bfloat16)
    summed = summed_on_arrival(partials, ("batch", "tensor"), 0)
    slot_out = summed[0].astype(jnp.bfloat16)
    returned = lax.all_to_all(slot_out, "expert", split_axis=0, concat_axis=0, tiled=True)
    returned = returned.reshape(experts, P_SIZE // batch_count, width_share)
    returned = collect(returned, "batch", 1)
    moe_out = jnp.dot(
        combine, returned.reshape(experts * P_SIZE, width_share), preferred_element_type=jnp.float32
    )
    return moe_out.astype(jnp.bfloat16)[None]


def solution(mesh):
    placed = (
        P("expert", "batch", "tensor"),
        P("tensor"),
        P("tensor", None),
        P("expert", None, ("batch", "tensor")),
        P("expert", None, ("batch", "tensor")),
        P("expert", ("batch", "tensor"), None),
    )
    return jax.shard_map(
        local, mesh=mesh, in_specs=placed, out_specs=P("expert", "batch", "tensor"), check_vma=False
    )
```

profile of v0, /device:TPU:0, one launch (start us, length us, event | category | flops | bytes accessed | tf_op | source)
XLA Modules:
  0.0 282.4 jit_solution(13784396119925911884)
XLA Ops:
  6.5 0.0 all-gather.2.cloned.1.call-start
  6.5 1.3 fusion.22
  7.9 0.7 convert_element_type.86
  8.5 0.0 copy-done
  8.5 1.5 convolution_bitcast_fusion
  10.0 0.1 copy.46
  10.2 2.5 broadcast_in_dim.12
  12.8 31.6 %all_to_all.41 = f32[4,1,131328]{2,1,0:T(1,128)S(1)} all-to-all(f32[4,1,131328]{2,1,0:T(1,128)S(1)} %broadcast_in_dim.12), channel_id=1, replica_groups=mesh['batch'=4,'expert'=8,'tensor'=4] {'tensor'}, dimensions={0} | all-to-all | bytes 4202496 | tf_op jit(solution)/shard_map/all_to_all | solution.py:12
  44.4 10.6 %reduce_sum.61 = f32[131328]{0:T(1024)} reduce(f32[4,1,131328]{2,1,0:T(1,128)S(1)} %all_to_all.41, f32[]{:T(128)} %constant.6.clone.1), dimensions={0,1}, to_apply=%region_1.0 | reduce | flops 393984 | bytes 2626564 | tf_op jit(solution)/shard_map/reduce_sum | solution.py:16
  55.0 0.7 fusion.35
  55.7 1.1 slice.52
  56.7 0.1 reshape.121
  56.8 0.2 multiply_reduce_fusion
  57.0 0.3 exponential_reduce_fusion
  57.4 9.6 %all_to_all.42 = f32[4,2,512]{2,1,0:T(2,128)S(1)} all-to-all(f32[4,2,512]{2,1,0:T(2,128)S(1)} %broadcast_in_dim.13), channel_id=1, replica_groups=mesh['batch'=4,'expert'=8,'tensor'=4] {'batch'}, dimensions={0} | all-to-all | bytes 32768 | tf_op jit(solution)/shard_map/all_to_all | solution.py:12
  67.2 0.2 fusion.32
  67.4 0.1 copy.31
  67.5 0.5 convolution_convert_fusion
  68.0 0.1 copy.57
  68.1 15.2 %all_to_all.43 = bf16[4,8,16,1024]{3,2,1,0:T(8,128)(2,1)S(1)} all-to-all(bf16[4,8,16,1024]{3,2,1,0:T(8,128)(2,1)S(1)} %bitcast.118), channel_id=1, replica_groups=mesh['batch'=4,'expert'=8,'tensor'=4] {'batch'}, dimensions={0} | all-to-all | bytes 2097152 | tf_op jit(solution)/shard_map/all_to_all | solution.py:65
  83.3 0.2 reduce_sum.64
  83.5 11.6 %all_to_all.44 = bf16[8,16,1024]{2,1,0:T(8,128)(2,1)S(1)} all-to-all(bf16[8,16,1024]{2,1,0:T(8,128)(2,1)S(1)} %reduce_sum.64), channel_id=1, replica_groups=mesh['batch'=4,'expert'=8,'tensor'=4] {'expert'}, dimensions={0} | all-to-all | bytes 524288 | tf_op jit(solution)/shard_map/all_to_all | solution.py:109
  95.1 0.1 broadcast_in_dim.14
  95.2 17.4 %all_to_all.45 = bf16[4,8,16,1024]{3,2,1,0:T(8,128)(2,1)S(1)} all-to-all(bf16[4,8,16,1024]{3,2,1,0:T(8,128)(2,1)S(1)} %broadcast_in_dim.14), channel_id=1, replica_groups=mesh['batch'=4,'expert'=8,'tensor'=4] {'batch'}, dimensions={0} | all-to-all | bytes 2097152 | tf_op jit(solution)/shard_map/all_to_all | solution.py:12
  112.6 1.0 copy.33
  113.7 0.0 all-gather.2.cloned.1.call-update
  113.7 13.1 %reshape.131 = bf16[896,4,1024]{2,1,0:T(4,128)(2,1)} reshape(bf16[1,896,4096]{2,1,0:T(8,128)(2,1)} %param.11) | data formatting | bytes 14680064 | tf_op jit(solution)/shard_map/reshape.6
  126.8 31.1 %all-gather.2.cloned.1.call-done = bf16[8,1,64,4096]{3,2,0,1:T(8,128)(2,1)} async-done(((bf16[8,1,64,1024]{3,2,0,1:T(8,128)(2,1)}), bf16[8,1,64,4096]{3,2,0,1:T(8,128)(2,1)}) %all-gather.2.cloned.1.call-update) | async-done | bytes 4194320 | tf_op jit(solution)/shard_map/all_gather | solution.py:114
  157.9 10.5 %fusion.4 = f32[8,64,896]{2,1,0:T(8,128)S(1)} fusion(bf16[1,4096,896]{2,1,0:T(8,128)(2,1)} %param.9, bf16[8,1,64,4096]{3,2,0,1:T(8,128)(2,1)} %all-gather.2.cloned.1.call-done), kind=kOutput, calls=%fused_computation.4 | convolution fusion | flops 3758096384 | bytes 13369344 | tf_op jit(solution)/shard_map/gxpd,xdf->gxpf/dot_general | solution.py:115
  168.5 0.0 slice-start.1
  168.5 7.8 %fusion.11 = bf16[8,1,64,896]{3,2,0,1:T(8,128)(2,1)S(1)} fusion(f32[8,64,896]{2,1,0:T(8,128)S(1)} %fusion.4, bf16[1,4096,896]{2,1,0:T(8,128)(2,1)} %param.10, bf16[8,1,64,4096]{3,2,0,1:T(8,128)(2,1)S(1)} %copy-done.4), kind=kOutput, calls=%fused_computation.10 | convolution fusion | flops 3760848896 | bytes 14286848 | tf_op jit(solution)/shard_map/gxpd,xdf->gxpf/dot_general | solution.py:118
  176.3 5.6 %fusion.8 = bf16[8,4,16,4,1024]{4,2,3,1,0:T(8,128)(2,1)S(1)} fusion(bf16[8,4,16,896,1]{3,2,4,1,0:T(8,128)(2,1)S(1)} %bitcast.130, bf16[896,4,1024,1,1]{2,1,0,4,3:T(4,128)(2,1)S(1)} %bitcast.113), kind=kOutput, calls=%fused_computation.8 | convolution fusion | flops 3760193536 | bytes 12451840 | tf_op jit(solution)/shard_map/gxbqf,xftd->btgxqd/dot_general | solution.py:124
  181.9 0.4 copy.35
  182.4 56.5 %all_to_all.46 = bf16[16,1,8,1,16,1024]{5,4,2,3,1,0:T(8,128)(2,1)} all-to-all(bf16[16,1,8,1,16,1024]{5,4,2,3,1,0:T(8,128)(2,1)S(1)} %copy.35), channel_id=1, replica_groups=mesh['batch'=4,'expert'=8,'tensor'=4] {'batch','tensor'}, dimensions={0} | all-to-all | bytes 8388608 | tf_op jit(solution)/shard_map/all_to_all | solution.py:65
  238.8 3.9 %reduce_sum.65 = bf16[8,16,1024]{2,1,0:T(8,128)(2,1)} reduce(bf16[16,1,8,1,16,1024]{5,4,2,3,1,0:T(8,128)(2,1)} %all_to_all.46, bf16[]{:T(256)} %constant.15.clone.1), dimensions={0,1,3}, to_apply=%region_7.8 | reduce | flops 1966080 | bytes 4456450 | tf_op jit(solution)/shard_map/reduce_sum | solution.py:66
  242.7 4.4 %all-to-all-start.6 = ((bf16[8,1,16,1024]{3,2,1,0:T(8,128)(2,1)}), bf16[8,1,16,1024]{3,2,1,0:T(8,128)(2,1)S(1)}, u32[]{:S(2)}, u32[]{:S(2)}) async-start(bf16[8,1,16,1024]{3,2,1,0:T(8,128)(2,1)} %bitcast.35), calls=%async_computation.6 | async-start | bytes 524288 | tf_op jit(solution)/shard_map/all_to_all | solution.py:132
  247.1 0.1 broadcast_bitcast_fusion
  247.2 0.9 copy.49
  248.1 1.0 copy.48
  249.1 0.9 copy.47
  250.0 4.6 %all-to-all-done.6 = bf16[8,1,16,1024]{3,2,1,0:T(8,128)(2,1)S(1)} async-done(((bf16[8,1,16,1024]{3,2,1,0:T(8,128)(2,1)}), bf16[8,1,16,1024]{3,2,1,0:T(8,128)(2,1)S(1)}, u32[]{:S(2)}, u32[]{:S(2)}) %all-to-all-start.6) | async-done | bytes 262176 | tf_op jit(solution)/shard_map/all_to_all | solution.py:132
  254.6 1.1 broadcast_in_dim.16
  255.7 3.5 %all-to-all-start.7 = ((bf16[4,8,16,1024]{3,2,1,0:T(8,128)(2,1)}), bf16[4,8,16,1024]{3,2,1,0:T(8,128)(2,1)S(1)}, u32[]{:S(2)}, u32[]{:S(2)}) async-start(bf16[4,8,16,1024]{3,2,1,0:T(8,128)(2,1)} %broadcast_in_dim.16), calls=%async_computation.7 | async-start | bytes 2097152 | tf_op jit(solution)/shard_map/all_to_all | solution.py:12
  259.3 1.5 divide_convert_fusion.1
  260.8 0.2 convert_element_type.89
  260.9 13.3 %all-to-all-done.7 = bf16[4,8,16,1024]{3,2,1,0:T(8,128)(2,1)S(1)} async-done(((bf16[4,8,16,1024]{3,2,1,0:T(8,128)(2,1)}), bf16[4,8,16,1024]{3,2,1,0:T(8,128)(2,1)S(1)}, u32[]{:S(2)}, u32[]{:S(2)}) %all-to-all-start.7) | async-done | bytes 1048608 | tf_op jit(solution)/shard_map/all_to_all | solution.py:12
  274.2 0.1 copy.36
  274.3 1.2 fusion.21
  (24 shorter events, 0.2 us)
Async XLA Ops:
  6.5 2.0 copy-start
  6.5 151.4 %all-gather.2.cloned.1.call-start = ((), (), s32[]{:S(2)}) async-start(), calls=%async_computation.8 | async-start | bytes 5242880 | tf_op jit(solution)/shard_map/all_gather | solution.py:114
  44.4 23.1 %copy-start.2 = (bf16[1,256,1024]{2,1,0:T(8,128)(2,1)S(1)}, bf16[1,256,1024]{2,1,0:T(8,128)(2,1)}, u32[]{:S(2)}) copy-start(bf16[1,256,1024]{2,1,0:T(8,128)(2,1)} %param.6) | copy-start | bytes 1572868
  157.9 10.5 %copy-start.4 = (bf16[8,1,64,4096]{3,2,0,1:T(8,128)(2,1)S(1)}, bf16[8,1,64,4096]{3,2,0,1:T(8,128)(2,1)}, u32[]{:S(2)}) copy-start(bf16[8,1,64,4096]{3,2,0,1:T(8,128)(2,1)} %all-gather.2.cloned.1.call-done) | copy-start | bytes 12582916
  157.9 18.3 %slice-start = ((s8[7340032]{0:T(1024)(128)(4,1)}), s8[4194304]{0:T(1024)(128)(4,1)S(1)}, s32[]{:S(2)}) async-start(s8[7340032]{0:T(1024)(128)(4,1)} %bitcast.111), calls=%async_computation.9 | async-start | bytes 8388608
  168.5 7.8 %slice-start.1 = ((s8[7340032]{0:T(1024)(128)(4,1)}), s8[3145728]{0:T(1024)(128)(4,1)S(1)}, s32[]{:S(2)}) async-start(s8[7340032]{0:T(1024)(128)(4,1)} %bitcast.111), calls=%async_computation.10 | async-start | bytes 6291456
  242.7 16.5 %copy-start.3 = (f32[131328]{0:T(1024)S(1)}, f32[131328]{0:T(1024)}, u32[]{:S(2)}) copy-start(f32[131328]{0:T(1024)} %reduce_sum.61) | copy-start | bytes 1575940
  242.7 11.9 %all-to-all-start.6 = ((bf16[8,1,16,1024]{3,2,1,0:T(8,128)(2,1)}), bf16[8,1,16,1024]{3,2,1,0:T(8,128)(2,1)S(1)}, u32[]{:S(2)}, u32[]{:S(2)}) async-start(bf16[8,1,16,1024]{3,2,1,0:T(8,128)(2,1)} %bitcast.35), calls=%async_computation.6 | async-start | bytes 524288 | tf_op jit(solution)/shard_map/all_to_all | solution.py:132
  254.6 21.0 %copy-start.1 = (bf16[1024,512]{1,0:T(8,128)(2,1)S(1)}, bf16[1024,512]{1,0:T(8,128)(2,1)}, u32[]{:S(2)}) copy-start(bf16[1024,512]{1,0:T(8,128)(2,1)} %param.8) | copy-start | bytes 3145732
  255.7 18.5 %all-to-all-start.7 = ((bf16[4,8,16,1024]{3,2,1,0:T(8,128)(2,1)}), bf16[4,8,16,1024]{3,2,1,0:T(8,128)(2,1)S(1)}, u32[]{:S(2)}, u32[]{:S(2)}) async-start(bf16[4,8,16,1024]{3,2,1,0:T(8,128)(2,1)} %broadcast_in_dim.16), calls=%async_computation.7 | async-start | bytes 2097152 | tf_op jit(solution)/shard_map/all_to_all | solution.py:12
Sparse Core Ops, SparseCore 0:
  113.8 44.0 all-gather.1
where the time goes:
time: 283 us; the launch traced here: 282 us
  blocking collectives  142 us (50%)
  waiting for transfers between devices  49 us (17%)
  matrix products  27.2 us (10%)
  local copies, waits for them, and re-layouts  23.2 us (8%)
  other arithmetic  19.6 us (7%)
  between operations  13.7 us (5%)
  starting transfers between devices  7.9 us (3%)
    all_to_all x2, blocking collectives, summed_on_arrival(): parts = lax.all_to_all(cut_along(x, dim, size), axis, 0, 0, tiled=True)  71.6 us
    all_to_all x3, blocking collectives, sent_to_all(): lax.all_to_all(jnp.broadcast_to(x[None], (size, *x.shape)), axis, 0, 0, t...  58.7 us
    all_gather x1, waiting for transfers between devices, local(): shard_piece = lax.all_gather(arrived, 'tensor', axis=3, tiled=True)  31.1 us
    all_to_all x1, waiting for transfers between devices, sent_to_all(): lax.all_to_all(jnp.broadcast_to(x[None], (size, *x.shape)), axis, 0, 0, t...  13.3 us
    another operation x1, local copies, waits for them, and re-layouts  13.1 us
    all_to_all x1, blocking collectives, local(): lax.all_to_all(quarter, 'expert', split_axis=0, concat_axis=0, tiled=True)  11.6 us
    reduce_sum x1, other arithmetic, of_everyone(): return sent_to_all(x, axis).sum(axis=0)  10.6 us
    dot_general x1, matrix products, local(): jnp.einsum('gxpd,xdf->gxpf', shard_piece, w_gate, preferred_element_type=...  10.5 us
  transfers between devices with their start and end apart: 3, of which 3 were waited for; matrix products, arithmetic and copies ran while one was open for 6% of the time, Pallas kernels for 0%

commit v1 on v0

v1 whole, which is shorter than its diff:
```python
import jax
import jax.numpy as jnp
from jax import lax
from jax.experimental import pallas as pl
from jax.experimental.pallas import tpu as pltpu
from jax.sharding import PartitionSpec as P


D = 4096
RING = 4
BF16 = jnp.bfloat16
F32 = jnp.float32


def near(v):
    return lax.rem(v + 2 * RING, RING)


class Net:
    def __init__(self, send_sems, recv_sems):
        self.send_sems, self.recv_sems = send_sems, recv_sems
        self.used, self.sent = 0, []

    def take(self, count=1):
        first = self.used
        self.used += count
        return first

    def copy(self, n, src, dst, target):
        return pltpu.make_async_remote_copy(
            src_ref=src,
            dst_ref=dst,
            send_sem=self.send_sems.at[n],
            recv_sem=self.recv_sems.at[n],
            device_id=target,
            device_id_type=pl.DeviceIdType.MESH,
        )

    def start(self, n, src, dst, target):
        one = self.copy(n, src, dst, target)
        one.start()
        self.sent.append(one)

    def arrived(self, n, dst, target):
        self.copy(n, dst, dst, target).wait_recv()

    def drain(self):
        for one in self.sent:
            one.wait_send()


class Gather:
    def __init__(self, net, axis, me, d, ref):
        self.net, self.axis, self.me, self.d, self.ref = net, axis, me, d, ref
        self.n = net.take(3)

    def to(self, d):
        return {self.axis: near(self.me + d)}

    def start(self):
        mine = self.ref(self.me)
        self.net.start(self.n, mine, mine, self.to(self.d))
        self.net.start(self.n + 1, mine, mine, self.to(-self.d))

    def relay(self):
        block = self.ref(near(self.me - self.d))
        self.net.arrived(self.n, block, self.to(self.d))
        self.net.start(self.n + 2, block, block, self.to(self.d))

    def direct(self):
        self.net.arrived(self.n + 1, self.ref(near(self.me + self.d)), self.to(self.d))

    def last(self):
        self.net.arrived(self.n + 2, self.ref(near(self.me + 2)), self.to(self.d))


class Scatter:
    def __init__(self, net, axis, me, d, part, buffers):
        self.net, self.axis, self.me, self.d, self.part = net, axis, me, d, part
        self.passing, self.direct_in, self.joined = buffers
        self.n = net.take(3)

    def to(self, d):
        return {self.axis: near(self.me + d)}

    def send_far(self):
        self.net.start(self.n, self.part(near(self.me + 2)), self.passing, self.to(self.d))

    def send_near(self):
        self.net.start(self.n + 1, self.part(near(self.me - self.d)), self.direct_in, self.to(-self.d))

    def relay(self):
        self.net.arrived(self.n, self.passing, self.to(self.d))
        term = self.part(near(self.me + self.d))
        total = term[...].astype(F32) + self.passing[...].astype(F32)
        term[...] = total.astype(term.dtype)
        self.net.start(self.n + 2, term, self.joined, self.to(self.d))

    def finish(self):
        self.net.arrived(self.n + 1, self.direct_in, self.to(self.d))
        self.net.arrived(self.n + 2, self.joined, self.to(self.d))
        mine = self.part(self.me)[...].astype(F32)
        return mine + self.direct_in[...].astype(F32) + self.joined[...].astype(F32)


def kernel(
    tok_in, gain, phi_in, wg_in, wu_in, wd_in, out,
    tok, phi, wg, wu, wd, sc,
    lp, l_in, sq_out, sq_in, st, qb, cb, qn,
    cs, c_in, si, xs, acc, hid, ys,
    a_in, a_sum, a2_in, b_in, b_sum, b2_in, so, rf,
    load_sems, send_sems, recv_sems,
):
    y = lax.axis_index("batch")
    e = lax.axis_index("expert")
    z = lax.axis_index("tensor")
    x, c = e // 2, lax.rem(e, 2)

    loads = [
        pltpu.make_async_copy(src, dst, load_sems.at[i])
        for i, (src, dst) in enumerate(
            ((tok_in, tok), (phi_in, phi), (wg_in, wg), (wu_in, wu), (wd_in, wd))
        )
    ]
    loads[0].start()
    loads[1].start()

    barrier = pltpu.get_barrier_semaphore()
    plane = [(dy, dz) for dy in range(RING) for dz in range(RING) if (dy, dz) != (0, 0)]
    across = [(dx, dc) for dx in (2, 1, 3, 0) for dc in range(2) if (dx, dc) != (0, 0)]

    def in_plane(dy, dz):
        return {"batch": near(y + dy), "tensor": near(z + dz)}

    def over_x(dx, dc):
        return {"expert": near(x + dx) * 2 + lax.rem(c + dc, 2)}

    peers = [in_plane(*step) for step in plane] + [over_x(*step) for step in across]
    for peer in peers:
        pl.semaphore_signal(
            barrier, inc=1, device_id=peer, device_id_type=pl.DeviceIdType.MESH
        )

    net = Net(send_sems, recv_sems)

    loads[0].wait()
    tokens_f = tok[...].astype(F32)
    sc[...] = (tokens_f * gain[...].astype(F32)).astype(BF16)
    squares = jnp.sum(tokens_f * tokens_f, axis=1, keepdims=True)
    rows = lp.shape[1]
    diagonal = lax.broadcasted_iota(jnp.int32, (rows, 128), 0) == lax.broadcasted_iota(
        jnp.int32, (rows, 128), 1
    )
    for b in range(RING):
        column = squares[b * rows : (b + 1) * rows]
        line = jnp.sum(jnp.where(diagonal, column, 0.0), axis=0, keepdims=True)
        sq_out[b] = jnp.broadcast_to(line, (8, 128))
    loads[1].wait()
    for b in range(RING):
        part = jnp.dot(
            sc[b * rows : (b + 1) * rows, :], phi[...], preferred_element_type=F32
        )
        lp[b] = part
    for one in loads[2:]:
        one.start()

    pl.semaphore_wait(barrier, len(peers))

    half = rows // 2
    logit_pieces = [
        Scatter(
            net, "tensor", z, d,
            lambda b, i=i: lp.at[b, pl.ds(i * half, half)],
            [l_in.at[k, i] for k in range(3)],
        )
        for i, d in enumerate((1, -1))
    ]
    for piece in logit_pieces:
        piece.send_far()
    first_sq = net.take(3)
    for k in range(3):
        to = near(z + k + 1)
        net.start(first_sq + k, sq_out.at[to], sq_in.at[k], {"tensor": to})
    for piece in logit_pieces:
        piece.send_near()
    for piece in logit_pieces:
        piece.relay()
    for k in range(3):
        net.arrived(first_sq + k, sq_in.at[k], {"tensor": near(z + k + 1)})
    sq = sq_out[z] + sq_in[0] + sq_in[1] + sq_in[2]
    sq_column = jnp.sum(jnp.where(diagonal, sq[0:1, :], 0.0), axis=1, keepdims=True)
    inv_rms = lax.rsqrt(sq_column / D + 1e-06)
    logits = jnp.concatenate([piece.finish() for piece in logit_pieces], axis=0) * inv_rms

    local_max = jnp.max(logits, axis=0, keepdims=True)
    raised = jnp.exp(logits - local_max)
    local_total = jnp.sum(raised, axis=0, keepdims=True)
    mine = st.at[y, z]
    for k in range(4):
        mine[k : k + 1, :] = local_max[:, k * 128 : (k + 1) * 128]
        mine[4 + k : 5 + k, :] = local_total[:, k * 128 : (k + 1) * 128]
    qb[z] = (raised * inv_rms).astype(BF16)
    first_st = net.take(len(plane))
    q_pieces = [
        Gather(net, "tensor", z, d, lambda b, i=i: qb.at[b, pl.ds(i * half, half)])
        for i, d in enumerate((1, -1))
    ]
    for piece in q_pieces:
        piece.start()
    for k, step in enumerate(plane):
        net.start(first_st + k, mine, mine, in_plane(*step))

    row_max = jnp.max(logits, axis=1, keepdims=True)
    row_raised = jnp.exp(logits - row_max)
    cb[z] = (row_raised / jnp.sum(row_raised, axis=1, keepdims=True)).astype(BF16)
    for piece in q_pieces:
        piece.relay()
    mix_pieces = [
        Gather(net, "tensor", z, d, lambda b, i=i: cb.at[b, pl.ds(i * half, half)])
        for i, d in enumerate((1, -1))
    ]
    for piece in mix_pieces:
        piece.start()
    for k, (dy, dz) in enumerate(plane):
        net.arrived(first_st + k, st.at[near(y - dy), near(z - dz)], in_plane(dy, dz))
    stats = st[...]
    maxima, totals = stats[:, :, 0:4, :], stats[:, :, 4:8, :]
    top = jnp.max(jnp.max(maxima, axis=1), axis=0)
    total = jnp.sum(jnp.sum(totals * jnp.exp(maxima - top[None, None]), axis=1), axis=0)
    factor = jnp.exp(st[y][:, 0:4, :] - top[None]) / total[None]
    for piece in q_pieces:
        piece.direct()
    for piece in q_pieces:
        piece.last()
    for b in range(RING):
        line = jnp.concatenate([factor[b, k : k + 1, :] for k in range(4)], axis=1)
        qn[b * rows : (b + 1) * rows, :] = (qb[b].astype(F32) * line).astype(BF16)
    for piece in mix_pieces:
        piece.relay()

    width = sc.shape[1]
    tile = 256

    @pl.loop(0, width // tile)
    def _(j):
        at = pl.ds(pl.multiple_of(j * tile, tile), tile)
        part = lax.dot_general(
            qn[...], sc[:, at], (((0,), (0,)), ((), ())), preferred_element_type=F32
        )
        cs[:, :, :, at] = part.astype(BF16).reshape(8, RING, 16, tile)

    pairs = [near(x + k) for k in (2, 1, 3, 0)]
    slot_pieces = [
        Scatter(
            net, "batch", y, d,
            lambda b, i=i: cs.at[pl.ds(2 * i, 2), b],
            [c_in.at[k, i] for k in range(3)],
        )
        for i, d in enumerate((1, -1, 1, -1))
    ]
    for piece in slot_pieces:
        piece.send_far()
    for piece in slot_pieces:
        piece.send_near()
    for piece in slot_pieces:
        piece.relay()
    for i, piece in enumerate(slot_pieces):
        si[2 * i : 2 * i + 2] = piece.finish().astype(BF16)

    def place(k, core):
        return xs.at[z, k // 2, y, pl.ds(lax.rem(k, 2) * 32 + core * 16, 16)]

    first_x = net.take(len(across))
    for n, (dx, dc) in enumerate(across):
        target = over_x(dx, dc)
        net.start(
            first_x + n, si.at[target["expert"]], place((RING - dx) % RING, c), target
        )
    place(0, c)[...] = si[e]

    def wait_x(k):
        for n, (dx, dc) in enumerate(across):
            if (RING - dx) % RING == k:
                net.arrived(first_x + n, place(k, lax.rem(c + dc, 2)), over_x(dx, dc))

    def strip(h, i):
        return pl.ds(i * 32, 32)

    a1 = [
        Gather(net, "batch", y, d, lambda b, i=i: xs.at[z, 0, b, pl.ds(i * 32, 32)])
        for i, d in enumerate((1, -1))
    ]
    b1 = [
        Gather(net, "tensor", z, d, lambda b, i=i: xs.at[b, 1, y, pl.ds(i * 32, 32)])
        for i, d in enumerate((1, -1))
    ]
    steps = (0, 3, 1, 2)
    ways = (1, 1, -1, -1)
    a2 = [
        Gather(net, "tensor", z, d, lambda b, j=j: xs.at[b, 0, near(y + j)])
        for j, d in zip(steps, ways)
    ]
    b2 = [
        Gather(net, "batch", y, d, lambda b, j=j: xs.at[near(z + j), 1, b])
        for j, d in zip(steps, ways)
    ]

    for k in (0, 1):
        wait_x(k)
        a1[k].start()
    for k in (2, 3):
        wait_x(k)
        b1[k - 2].start()
    a2[0].start()
    b2[0].start()
    for stage in (a1, b1):
        for piece in stage:
            piece.relay()
    for stage, later in ((a1, a2), (b1, b2)):
        for piece in stage:
            piece.direct()
        later[1].start()
        later[2].start()
    for stage, later in ((a1, a2), (b1, b2)):
        for piece in stage:
            piece.last()
        later[3].start()

    loads[2].wait()
    loads[3].wait()
    share = acc.shape[0]

    def raise_rows(h, b, first):
        deep = pl.ds(pl.multiple_of(b * width, width), width)
        block = xs[b, h].reshape(RING * 64, width)

        @pl.loop(0, share)
        def _(j):
            at = pl.ds(pl.multiple_of(j * 128, 128), 128)
            both = jnp.concatenate([wg[deep, at], wu[deep, at]], axis=1)
            part = jnp.dot(block, both, preferred_element_type=F32)
            if first:
                acc[j, h] = part
            else:
                acc[j, h] = acc[j, h] + part

    def close_rows(h):
        @pl.loop(0, share)
        def _(j):
            at = pl.ds(pl.multiple_of(j * 128, 128), 128)
            gate, up = acc[j, h][:, :128], acc[j, h][:, 128:]
            hid[h, :, at] = (gate / (1.0 + jnp.exp(-gate)) * up).astype(BF16)

    raise_rows(0, z, True)
    a2[0].relay()
    b2[0].relay()
    a2[2].relay()
    b2[2].relay()
    b2[0].direct()
    a2[1].relay()
    b2[1].relay()
    b2[0].last()
    raise_rows(1, z, True)
    a2[3].relay()
    b2[3].relay()
    for piece in a2:
        piece.direct()
    raise_rows(0, near(z - 1), False)
    raise_rows(0, near(z + 1), False)
    b2[1].direct()
    b2[1].last()
    raise_rows(1, near(z - 1), False)
    b2[2].direct()
    b2[2].last()
    raise_rows(1, near(z + 1), False)
    for piece in a2:
        piece.last()
    raise_rows(0, near(z + 2), False)
    close_rows(0)

    loads[4].wait()

    def lower_rows(h, b):
        @pl.loop(0, width // tile)
        def _(j):
            inside = pl.ds(pl.multiple_of(j * tile, tile), tile)
            at = pl.ds(pl.multiple_of(b * width + j * tile, tile), tile)
            part = jnp.dot(hid[h], wd[:, at], preferred_element_type=F32)
            ys[b, h, :, :, inside] = part.astype(BF16).reshape(RING, 64, tile)

    order = (2, 1, 3, 0)
    sides = (1, -1, 1, -1)
    ra1 = [
        Scatter(
            net, "tensor", z, d,
            lambda b, j=j: ys.at[b, 0, near(y + j)],
            [a_in.at[k, i] for k in range(3)],
        )
        for i, (j, d) in enumerate(zip(order, sides))
    ]
    rb1 = [
        Scatter(
            net, "batch", y, d,
            lambda b, j=j: ys.at[near(z + j), 1, b],
            [b_in.at[k, i] for k in range(3)],
        )
        for i, (j, d) in enumerate(zip(order, sides))
    ]
    ra2 = [
        Scatter(
            net, "batch", y, d,
            lambda b, i=i: a_sum.at[b, pl.ds(i * 32, 32)],
            [a2_in.at[k, i] for k in range(3)],
        )
        for i, d in enumerate((1, -1))
    ]
    rb2 = [
        Scatter(
            net, "tensor", z, d,
            lambda b, i=i: b_sum.at[b, pl.ds(i * 32, 32)],
            [b2_in.at[k, i] for k in range(3)],
        )
        for i, d in enumerate((1, -1))
    ]

    lower_rows(0, near(z + 2))
    for piece in ra1:
        piece.send_far()
    b2[3].direct()
    b2[3].last()
    raise_rows(1, near(z + 2), False)
    close_rows(1)
    lower_rows(1, near(z + 2))
    rb1[0].send_far()
    rb1[0].send_near()
    lower_rows(0, near(z + 1))
    ra1[1].send_near()
    ra1[3].send_near()
    lower_rows(1, near(z + 1))
    rb1[1].send_far()
    rb1[1].send_near()
    lower_rows(0, near(z - 1))
    ra1[0].send_near()
    ra1[2].send_near()
    lower_rows(1, near(z - 1))
    rb1[2].send_far()
    rb1[2].send_near()
    ra1[0].relay()
    ra1[1].relay()
    rb1[0].relay()
    lower_rows(1, z)
    rb1[3].send_far()
    rb1[3].send_near()
    lower_rows(0, z)
    rb1[1].relay()
    ra1[2].relay()
    ra1[3].relay()
    rb1[2].relay()
    rb1[3].relay()

    def close_sum(pieces, n, sums, me):
        sums[near(me + order[n])] = pieces[n].finish().astype(BF16)

    close_sum(ra1, 0, a_sum, y)
    for piece in ra2:
        piece.send_far()
    close_sum(rb1, 0, b_sum, z)
    for piece in rb2:
        piece.send_far()
    for n in (1, 2):
        close_sum(ra1, n, a_sum, y)
        close_sum(rb1, n, b_sum, z)
    for piece in (*ra2, *rb2):
        piece.send_near()
    for piece in (*ra2, *rb2):
        piece.relay()
    close_sum(ra1, 3, a_sum, y)
    close_sum(rb1, 3, b_sum, z)

    first_back = net.take(len(across))
    backs = {step: first_back + n for n, step in enumerate(across)}
    for k, piece in enumerate((*ra2, *rb2)):
        so[k] = piece.finish().astype(BF16)
        for dc in range(2):
            core = lax.rem(c + dc, 2)
            mine = so.at[k, pl.ds(core * 16, 16)]
            if (k, dc) == (0, 0):
                rf[e, y] = mine[...]
            else:
                net.start(backs[k, dc], mine, rf.at[e, y], over_x(k, dc))

    out_pieces = [
        Gather(net, "batch", y, d, lambda b, k=k: rf.at[pl.ds(2 * near(x - k), 2), b])
        for k, d in enumerate((1, -1, 1, -1))
    ]
    for k, piece in enumerate(out_pieces):
        for dc in range(2):
            if (k, dc) != (0, 0):
                source = near(x - k) * 2 + lax.rem(c + dc, 2)
                net.arrived(backs[k, dc], rf.at[source, y], over_x(k, dc))
        piece.start()
    for piece in mix_pieces:
        piece.direct()
        piece.last()
    for piece in out_pieces:
        piece.relay()
    for piece in out_pieces:
        piece.direct()
    for piece in out_pieces:
        piece.last()

    @pl.loop(0, width // tile)
    def _(j):
        at = pl.ds(pl.multiple_of(j * tile, tile), tile)
        rows_in = rf[:, :, :, at].reshape(512, tile)
        mix = cb[...].reshape(RING * rows, 512)
        out[:, at] = jnp.dot(mix, rows_in, preferred_element_type=F32).astype(BF16)

    net.drain()


MESSAGES = 146


def local(tokens, gain, phi, w_gate, w_up, w_down):
    share = w_gate.shape[2]
    width = tokens.shape[2]
    count = tokens.shape[1]
    rows = count // RING
    slots = phi.shape[1]
    vmem = pltpu.VMEM
    scratch = [
        vmem((count, width), BF16),
        vmem((width, slots), BF16),
        vmem((D, share), BF16),
        vmem((D, share), BF16),
        vmem((share, D), BF16),
        vmem((count, width), BF16),
        vmem((RING, rows, slots), F32),
        vmem((3, 2, rows // 2, slots), F32),
        vmem((RING, 8, 128), F32),
        vmem((3, 8, 128), F32),
        vmem((RING, RING, 8, 128), F32),
        vmem((RING, rows, slots), BF16),
        vmem((RING, rows, slots), BF16),
        vmem((count, slots), BF16),
        vmem((8, RING, 16, width), BF16),
        vmem((3, 4, 2, 16, width), BF16),
        vmem((8, 16, width), BF16),
        vmem((RING, 2, RING, 64, width), BF16),
        vmem((share // 128, 2, 256, 256), F32),
        vmem((2, 256, share), BF16),
        vmem((RING, 2, RING, 64, width), BF16),
        vmem((3, 4, 64, width), BF16),
        vmem((RING, 64, width), BF16),
        vmem((3, 2, 32, width), BF16),
        vmem((3, 4, 64, width), BF16),
        vmem((RING, 64, width), BF16),
        vmem((3, 2, 32, width), BF16),
        vmem((4, 32, width), BF16),
        vmem((8, RING, 16, width), BF16),
        pltpu.SemaphoreType.DMA((5,)),
        pltpu.SemaphoreType.DMA((MESSAGES,)),
        pltpu.SemaphoreType.DMA((MESSAGES,)),
    ]
    anywhere = pl.BlockSpec(memory_space=pl.ANY)
    inside = pl.BlockSpec(memory_space=vmem)
    out = pl.pallas_call(
        kernel,
        out_shape=jax.ShapeDtypeStruct((count, width), BF16),
        in_specs=[anywhere, inside, anywhere, anywhere, anywhere, anywhere],
        out_specs=inside,
        scratch_shapes=scratch,
        compiler_params=pltpu.CompilerParams(
            collective_id=0, has_side_effects=True, vmem_limit_bytes=60 << 20
        ),
        name="soft_moe",
    )(tokens[0], gain[None], phi, w_gate[0], w_up[0], w_down[0])
    return out[None]


def solution(mesh):
    placed = (
        P("expert", "batch", "tensor"),
        P("tensor"),
        P("tensor", None),
        P("expert", None, ("batch", "tensor")),
        P("expert", None, ("batch", "tensor")),
        P("expert", ("batch", "tensor"), None),
    )
    return jax.shard_map(
        local, mesh=mesh, in_specs=placed, out_specs=P("expert", "batch", "tensor"), check_vma=False
    )
```

time: 283 us -> 124 us (0.44)
  blocking collectives: 142 us -> 0 us
  Pallas kernels: 0 us -> 119 us
  waiting for transfers between devices: 49 us -> 0 us
  matrix products: 27.2 us -> 0 us
  local copies, waits for them, and re-layouts: 23.2 us -> 3.15 us
  other arithmetic: 19.6 us -> 0 us
  between operations: 13.7 us -> 0.01 us
  starting transfers between devices: 7.9 us -> 0 us
    all_to_all x6 -> x0, blocking collectives: 142 us -> none  [the longest x2 71.6 us: summed_on_arrival(): parts = lax.all_to_all(cut_along(x, dim, size), axis, 0, 0, tiled=True)]
    pallas_call x0 -> x1, Pallas kernels: none -> 119 us  [local(): pl.pallas_call(kernel, out_shape=jax.ShapeDtypeStruct((count, width), BF1...]
    all_gather x1 -> x0, waiting for transfers between devices: 31.1 us -> none  [local(): shard_piece = lax.all_gather(arrived, 'tensor', axis=3, tiled=True)]
    dot_general x6 -> x0, matrix products: 27.2 us -> none  [the longest x1 10.5 us: local(): jnp.einsum('gxpd,xdf->gxpf', shard_piece, w_gate, preferred_element_type=...]
    all_to_all x2 -> x0, waiting for transfers between devices: 17.8 us -> none  [the longest x1 13.3 us: sent_to_all(): lax.all_to_all(jnp.broadcast_to(x[None], (size, *x.shape)), axis, 0, 0, t...]
    reduce_sum x5 -> x0, other arithmetic: 16.3 us -> none  [the longest x1 10.6 us: of_everyone(): return sent_to_all(x, axis).sum(axis=0)]
    another operation x1 -> x0, local copies, waits for them, and re-layouts: 13.1 us -> none
    all_to_all x2 -> x0, starting transfers between devices: 7.9 us -> none  [the longest x1 4.39 us: local(): lax.all_to_all(slot_out, 'expert', split_axis=0, concat_axis=0, tiled=True)]
  transfers between devices with their start and end apart: 3 -> 0, of which waited for: 3 -> 0; matrix products, arithmetic and copies ran while one was open for 6% -> 0% of each run, Pallas kernels for 0% -> 0%
where the time goes in v1:
time: 124 us; the launch traced here: 122 us
  Pallas kernels  119 us (96%)
  local copies, waits for them, and re-layouts  3.15 us (3%)
    pallas_call x1, Pallas kernels, local(): pl.pallas_call(kernel, out_shape=jax.ShapeDtypeStruct((count, width), BF1...  119 us

profile of v1, /device:TPU:0, one launch (start us, length us, event | category | flops | bytes accessed | tf_op | source)
XLA Modules:
  0.0 122.5 jit_solution(6201993713101755336)
XLA Ops:
  0.0 1.3 %broadcast_in_dim.6.gain = bf16[1,1024]{1,0:T(2,128)(2,1)} reshape(bf16[1024]{0:T(1024)(128)(2,1)} %param.7) | data formatting | bytes 4096 | tf_op jit(solution)/shard_map/broadcast_in_dim | solution.py:578
  1.3 119.3 %soft_moe.1 = bf16[256,1024]{1,0:T(8,128)(2,1)} custom-call(bf16[256,1024]{1,0:T(8,128)(2,1)} %bitcast.9, bf16[1,1024]{1,0:T(2,128)(2,1)} %broadcast_in_dim.6.gain, bf16[1024,512]{1,0:T(8,128)(2,1)} %phi_in.1, bf16[4096,896]{1,0:T(8,128)(2,1)} %bitcast.5, bf16[4096,896]{1,0:T(8,128)(2,1)} %bitcast.6, bf16[896,4096]{1,0:T(8,128)(2,1)} %bitcast.7), custom_call_target="tpu_custom_call" | custom-call | tf_op jit(solution)/shard_map/soft_moe/pallas_call | solution.py:568
  120.6 1.9 %copy.8 = bf16[1,256,1024]{2,1,0:T(8,128)(2,1)} copy(bf16[1,256,1024]{2,1,0:T(8,128)(2,1)} %bitcast.8) | data formatting | bytes 1048576

commit v2 on v1

--- a/solution.py
+++ b/solution.py
@@ -104,11 +104,11 @@
 
 
 def kernel(
-    tok_in, gain, phi_in, wg_in, wu_in, wd_in, out,
-    tok, phi, wg, wu, wd, sc,
-    lp, l_in, sq_out, sq_in, st, qb, cb, qn,
-    cs, c_in, si, xs, acc, hid, ys,
-    a_in, a_sum, a2_in, b_in, b_sum, b2_in, so, rf,
+    tok_in, gain, phi_in, wg_in, wu_in, wd_in, cb, rf,
+    tok, phi, wg, wu, wd, tg,
+    lp, l_in, sq_out, sq_in, st, qo, qg, qt,
+    si, xs, acc, hid, ys,
+    a_in, a_sum, a2_in, b_in, b_sum, b2_in, so,
     load_sems, send_sems, recv_sems,
 ):
     y = lax.axis_index("batch")
@@ -143,11 +143,14 @@
 
     net = Net(send_sems, recv_sems)
 
+    rows = lp.shape[1]
+    width = tok.shape[1]
+    wide = jnp.concatenate([gain[k : k + 1, :] for k in range(width // 128)], axis=1)
     loads[0].wait()
     tokens_f = tok[...].astype(F32)
-    sc[...] = (tokens_f * gain[...].astype(F32)).astype(BF16)
+    scaled = (tokens_f * wide.astype(F32)).astype(BF16)
+    tg[y] = scaled
     squares = jnp.sum(tokens_f * tokens_f, axis=1, keepdims=True)
-    rows = lp.shape[1]
     diagonal = lax.broadcasted_iota(jnp.int32, (rows, 128), 0) == lax.broadcasted_iota(
         jnp.int32, (rows, 128), 1
     )
@@ -158,7 +161,7 @@
     loads[1].wait()
     for b in range(RING):
         part = jnp.dot(
-            sc[b * rows : (b + 1) * rows, :], phi[...], preferred_element_type=F32
+            scaled[b * rows : (b + 1) * rows, :], phi[...], preferred_element_type=F32
         )
         lp[b] = part
     for one in loads[2:]:
@@ -174,6 +177,10 @@
             [l_in.at[k, i] for k in range(3)],
         )
         for i, d in enumerate((1, -1))
+    ]
+    token_pieces = [
+        Gather(net, "batch", y, d, lambda b, i=i: tg.at[b, pl.ds(i * rows, rows)])
+        for i, d in enumerate((1, -1, 1, -1))
     ]
     for piece in logit_pieces:
         piece.send_far()
@@ -183,8 +190,11 @@
         net.start(first_sq + k, sq_out.at[to], sq_in.at[k], {"tensor": to})
     for piece in logit_pieces:
         piece.send_near()
+    token_pieces[0].start()
+    token_pieces[1].start()
     for piece in logit_pieces:
         piece.relay()
+    token_pieces[2].start()
     for k in range(3):
         net.arrived(first_sq + k, sq_in.at[k], {"tensor": near(z + k + 1)})
     sq = sq_out[z] + sq_in[0] + sq_in[1] + sq_in[2]
@@ -192,80 +202,90 @@
     inv_rms = lax.rsqrt(sq_column / D + 1e-06)
     logits = jnp.concatenate([piece.finish() for piece in logit_pieces], axis=0) * inv_rms
 
+    lane = lax.broadcasted_iota(jnp.int32, (rows, 128), 1)
+    quarters = []
+    for q in range(RING):
+        made = jnp.zeros((rows, 128), F32)
+        for n in range(8):
+            source = logits[:, n // 2 * 128 : n // 2 * 128 + 128]
+            shift = (n * 16 - n % 2 * 64 - q * 16) % 128
+            moved = pltpu.roll(source, shift, 1) if shift else source
+            made = jnp.where((lane >= n * 16) & (lane < n * 16 + 16), moved, made)
+        quarters.append(made)
+    logits = jnp.concatenate(quarters, axis=1)
+
     local_max = jnp.max(logits, axis=0, keepdims=True)
     raised = jnp.exp(logits - local_max)
     local_total = jnp.sum(raised, axis=0, keepdims=True)
     mine = st.at[y, z]
-    for k in range(4):
+    for k in range(RING):
         mine[k : k + 1, :] = local_max[:, k * 128 : (k + 1) * 128]
         mine[4 + k : 5 + k, :] = local_total[:, k * 128 : (k + 1) * 128]
-    qb[z] = (raised * inv_rms).astype(BF16)
+    factor = (raised * inv_rms).astype(BF16)
+    for k in range(RING):
+        qo[k] = factor[:, k * 128 : (k + 1) * 128]
+    qg[z, y] = qo[y]
+    first_q = net.take(3)
+    for k in (1, 0, 2):
+        to = near(y + k + 1)
+        net.start(first_q + k, qo.at[to], qg.at[z, y], {"batch": to})
     first_st = net.take(len(plane))
-    q_pieces = [
-        Gather(net, "tensor", z, d, lambda b, i=i: qb.at[b, pl.ds(i * half, half)])
-        for i, d in enumerate((1, -1))
-    ]
-    for piece in q_pieces:
-        piece.start()
     for k, step in enumerate(plane):
         net.start(first_st + k, mine, mine, in_plane(*step))
+    token_pieces[3].start()
+    token_pieces[0].relay()
+    token_pieces[1].relay()
 
     row_max = jnp.max(logits, axis=1, keepdims=True)
     row_raised = jnp.exp(logits - row_max)
     cb[z] = (row_raised / jnp.sum(row_raised, axis=1, keepdims=True)).astype(BF16)
+    for k in range(3):
+        net.arrived(first_q + k, qg.at[z, near(y - k - 1)], {"batch": near(y + k + 1)})
+    q_pieces = [
+        Gather(net, "tensor", z, d, lambda b, i=i: qg.at[b, pl.ds(i * 2, 2)])
+        for i, d in enumerate((1, -1))
+    ]
     for piece in q_pieces:
-        piece.relay()
-    mix_pieces = [
-        Gather(net, "tensor", z, d, lambda b, i=i: cb.at[b, pl.ds(i * half, half)])
-        for i, d in enumerate((1, -1))
-    ]
-    for piece in mix_pieces:
         piece.start()
     for k, (dy, dz) in enumerate(plane):
         net.arrived(first_st + k, st.at[near(y - dy), near(z - dz)], in_plane(dy, dz))
-    stats = st[...]
-    maxima, totals = stats[:, :, 0:4, :], stats[:, :, 4:8, :]
-    top = jnp.max(jnp.max(maxima, axis=1), axis=0)
-    total = jnp.sum(jnp.sum(totals * jnp.exp(maxima - top[None, None]), axis=1), axis=0)
-    factor = jnp.exp(st[y][:, 0:4, :] - top[None]) / total[None]
+    maxima = st[:, :, pl.ds(y, 1), :]
+    totals = st[:, :, pl.ds(RING + y, 1), :]
+    top = jnp.max(jnp.max(maxima, axis=1, keepdims=True), axis=0, keepdims=True)
+    weights = jnp.exp(maxima - top)
+    total = jnp.sum(jnp.sum(totals * weights, axis=1, keepdims=True), axis=0, keepdims=True)
+    weights = weights / total
+    for piece in q_pieces:
+        piece.relay()
+    token_pieces[2].relay()
+    token_pieces[3].relay()
+    mix_pieces = [
+        Gather(net, "tensor", z, d, lambda b, i=i: cb.at[b, pl.ds(i * half, half)])
+        for i, d in enumerate((1, -1))
+    ]
     for piece in q_pieces:
         piece.direct()
     for piece in q_pieces:
         piece.last()
     for b in range(RING):
-        line = jnp.concatenate([factor[b, k : k + 1, :] for k in range(4)], axis=1)
-        qn[b * rows : (b + 1) * rows, :] = (qb[b].astype(F32) * line).astype(BF16)
+        scaled_q = jnp.concatenate(
+            [qg[k, b].astype(F32) * weights[b, k] for k in range(RING)], axis=0
+        )
+        qt[:, b * RING * rows : (b + 1) * RING * rows] = scaled_q.T.astype(BF16)
+    for piece in token_pieces:
+        piece.direct()
+    for piece in token_pieces:
+        piece.last()
     for piece in mix_pieces:
-        piece.relay()
-
-    width = sc.shape[1]
+        piece.start()
+
     tile = 256
-
-    @pl.loop(0, width // tile)
-    def _(j):
-        at = pl.ds(pl.multiple_of(j * tile, tile), tile)
-        part = lax.dot_general(
-            qn[...], sc[:, at], (((0,), (0,)), ((), ())), preferred_element_type=F32
-        )
-        cs[:, :, :, at] = part.astype(BF16).reshape(8, RING, 16, tile)
-
-    pairs = [near(x + k) for k in (2, 1, 3, 0)]
-    slot_pieces = [
-        Scatter(
-            net, "batch", y, d,
-            lambda b, i=i: cs.at[pl.ds(2 * i, 2), b],
-            [c_in.at[k, i] for k in range(3)],
-        )
-        for i, d in enumerate((1, -1, 1, -1))
-    ]
-    for piece in slot_pieces:
-        piece.send_far()
-    for piece in slot_pieces:
-        piece.send_near()
-    for piece in slot_pieces:
-        piece.relay()
-    for i, piece in enumerate(slot_pieces):
-        si[2 * i : 2 * i + 2] = piece.finish().astype(BF16)
+    for j in range(width // tile):
+        at = pl.ds(j * tile, tile)
+        part = jnp.dot(
+            qt[...], tg[:, :, at].reshape(qt.shape[1], tile), preferred_element_type=F32
+        )
+        si[:, :, at] = part.astype(BF16).reshape(8, 16, tile)
 
     def place(k, core):
         return xs.at[z, k // 2, y, pl.ds(lax.rem(k, 2) * 32 + core * 16, 16)]
@@ -282,9 +302,6 @@
         for n, (dx, dc) in enumerate(across):
             if (RING - dx) % RING == k:
                 net.arrived(first_x + n, place(k, lax.rem(c + dc, 2)), over_x(dx, dc))
-
-    def strip(h, i):
-        return pl.ds(i * 32, 32)
 
     a1 = [
         Gather(net, "batch", y, d, lambda b, i=i: xs.at[z, 0, b, pl.ds(i * 32, 32)])
@@ -311,6 +328,8 @@
     for k in (2, 3):
         wait_x(k)
         b1[k - 2].start()
+    for piece in mix_pieces:
+        piece.relay()
     a2[0].start()
     b2[0].start()
     for stage in (a1, b1):
@@ -330,28 +349,24 @@
     loads[3].wait()
     share = acc.shape[0]
 
-    def raise_rows(h, b, first):
+    def raise_rows(b, halves, first=False, last=False):
         deep = pl.ds(pl.multiple_of(b * width, width), width)
-        block = xs[b, h].reshape(RING * 64, width)
-
-        @pl.loop(0, share)
-        def _(j):
-            at = pl.ds(pl.multiple_of(j * 128, 128), 128)
+        lo, hi = halves[0], halves[-1] + 1
+        count = (hi - lo) * RING * 64
+        block = xs[b, lo:hi].reshape(count, width)
+        for j in range(share):
+            at = pl.ds(j * 128, 128)
             both = jnp.concatenate([wg[deep, at], wu[deep, at]], axis=1)
             part = jnp.dot(block, both, preferred_element_type=F32)
-            if first:
-                acc[j, h] = part
+            if not first:
+                part = acc[j, lo:hi].reshape(count, 256) + part
+            if last:
+                gate, up = part[:, :128], part[:, 128:]
+                hid[:, at] = (gate / (1.0 + jnp.exp(-gate)) * up).astype(BF16)
             else:
-                acc[j, h] = acc[j, h] + part
-
-    def close_rows(h):
-        @pl.loop(0, share)
-        def _(j):
-            at = pl.ds(pl.multiple_of(j * 128, 128), 128)
-            gate, up = acc[j, h][:, :128], acc[j, h][:, 128:]
-            hid[h, :, at] = (gate / (1.0 + jnp.exp(-gate)) * up).astype(BF16)
-
-    raise_rows(0, z, True)
+                acc[j, lo:hi] = part.reshape(hi - lo, RING * 64, 256)
+
+    raise_rows(z, (0,), first=True)
     a2[0].relay()
     b2[0].relay()
     a2[2].relay()
@@ -360,33 +375,31 @@
     a2[1].relay()
     b2[1].relay()
     b2[0].last()
-    raise_rows(1, z, True)
+    raise_rows(z, (1,), first=True)
     a2[3].relay()
     b2[3].relay()
     for piece in a2:
         piece.direct()
-    raise_rows(0, near(z - 1), False)
-    raise_rows(0, near(z + 1), False)
     b2[1].direct()
     b2[1].last()
-    raise_rows(1, near(z - 1), False)
+    raise_rows(near(z - 1), (0, 1))
     b2[2].direct()
     b2[2].last()
-    raise_rows(1, near(z + 1), False)
+    raise_rows(near(z + 1), (0, 1))
     for piece in a2:
         piece.last()
-    raise_rows(0, near(z + 2), False)
-    close_rows(0)
+    b2[3].direct()
+    b2[3].last()
+    raise_rows(near(z + 2), (0, 1), last=True)
 
     loads[4].wait()
 
-    def lower_rows(h, b):
-        @pl.loop(0, width // tile)
-        def _(j):
-            inside = pl.ds(pl.multiple_of(j * tile, tile), tile)
+    def lower_rows(b):
+        for j in range(width // tile):
+            inside = pl.ds(j * tile, tile)
             at = pl.ds(pl.multiple_of(b * width + j * tile, tile), tile)
-            part = jnp.dot(hid[h], wd[:, at], preferred_element_type=F32)
-            ys[b, h, :, :, inside] = part.astype(BF16).reshape(RING, 64, tile)
+            part = jnp.dot(hid[...], wd[:, at], preferred_element_type=F32)
+            ys[b, :, :, :, inside] = part.astype(BF16).reshape(2, RING, 64, tile)
 
     order = (2, 1, 3, 0)
     sides = (1, -1, 1, -1)
@@ -423,35 +436,27 @@
         for i, d in enumerate((1, -1))
     ]
 
-    lower_rows(0, near(z + 2))
+    lower_rows(near(z + 2))
     for piece in ra1:
         piece.send_far()
-    b2[3].direct()
-    b2[3].last()
-    raise_rows(1, near(z + 2), False)
-    close_rows(1)
-    lower_rows(1, near(z + 2))
     rb1[0].send_far()
     rb1[0].send_near()
-    lower_rows(0, near(z + 1))
+    lower_rows(near(z + 1))
     ra1[1].send_near()
     ra1[3].send_near()
-    lower_rows(1, near(z + 1))
     rb1[1].send_far()
     rb1[1].send_near()
-    lower_rows(0, near(z - 1))
+    lower_rows(near(z - 1))
     ra1[0].send_near()
     ra1[2].send_near()
-    lower_rows(1, near(z - 1))
     rb1[2].send_far()
     rb1[2].send_near()
+    lower_rows(z)
+    rb1[3].send_far()
+    rb1[3].send_near()
     ra1[0].relay()
     ra1[1].relay()
     rb1[0].relay()
-    lower_rows(1, z)
-    rb1[3].send_far()
-    rb1[3].send_near()
-    lower_rows(0, z)
     rb1[1].relay()
     ra1[2].relay()
     ra1[3].relay()
@@ -485,23 +490,20 @@
             core = lax.rem(c + dc, 2)
             mine = so.at[k, pl.ds(core * 16, 16)]
             if (k, dc) == (0, 0):
-                rf[e, y] = mine[...]
+                rf[y, e] = mine[...]
             else:
-                net.start(backs[k, dc], mine, rf.at[e, y], over_x(k, dc))
+                net.start(backs[k, dc], mine, rf.at[y, e], over_x(k, dc))
 
     out_pieces = [
-        Gather(net, "batch", y, d, lambda b, k=k: rf.at[pl.ds(2 * near(x - k), 2), b])
+        Gather(net, "batch", y, d, lambda b, k=k: rf.at[b, pl.ds(2 * near(x - k), 2)])
         for k, d in enumerate((1, -1, 1, -1))
     ]
     for k, piece in enumerate(out_pieces):
         for dc in range(2):
             if (k, dc) != (0, 0):
                 source = near(x - k) * 2 + lax.rem(c + dc, 2)
-                net.arrived(backs[k, dc], rf.at[source, y], over_x(k, dc))
+                net.arrived(backs[k, dc], rf.at[y, source], over_x(k, dc))
         piece.start()
-    for piece in mix_pieces:
-        piece.direct()
-        piece.last()
     for piece in out_pieces:
         piece.relay()
     for piece in out_pieces:
@@ -509,17 +511,13 @@
     for piece in out_pieces:
         piece.last()
 
-    @pl.loop(0, width // tile)
-    def _(j):
-        at = pl.ds(pl.multiple_of(j * tile, tile), tile)
-        rows_in = rf[:, :, :, at].reshape(512, tile)
-        mix = cb[...].reshape(RING * rows, 512)
-        out[:, at] = jnp.dot(mix, rows_in, preferred_element_type=F32).astype(BF16)
-
+    for piece in mix_pieces:
+        piece.direct()
+        piece.last()
     net.drain()
 
 
-MESSAGES = 146
+MESSAGES = 149
 
 
 def local(tokens, gain, phi, w_gate, w_up, w_down):
@@ -535,21 +533,19 @@
         vmem((D, share), BF16),
         vmem((D, share), BF16),
         vmem((share, D), BF16),
-        vmem((count, width), BF16),
+        vmem((RING, count, width), BF16),
         vmem((RING, rows, slots), F32),
         vmem((3, 2, rows // 2, slots), F32),
         vmem((RING, 8, 128), F32),
         vmem((3, 8, 128), F32),
         vmem((RING, RING, 8, 128), F32),
-        vmem((RING, rows, slots), BF16),
-        vmem((RING, rows, slots), BF16),
-        vmem((count, slots), BF16),
-        vmem((8, RING, 16, width), BF16),
-        vmem((3, 4, 2, 16, width), BF16),
+        vmem((RING, rows, 128), BF16),
+        vmem((RING, RING, rows, 128), BF16),
+        vmem((128, RING * count), BF16),
         vmem((8, 16, width), BF16),
         vmem((RING, 2, RING, 64, width), BF16),
         vmem((share // 128, 2, 256, 256), F32),
-        vmem((2, 256, share), BF16),
+        vmem((512, share), BF16),
         vmem((RING, 2, RING, 64, width), BF16),
         vmem((3, 4, 64, width), BF16),
         vmem((RING, 64, width), BF16),
@@ -558,25 +554,30 @@
         vmem((RING, 64, width), BF16),
         vmem((3, 2, 32, width), BF16),
         vmem((4, 32, width), BF16),
-        vmem((8, RING, 16, width), BF16),
         pltpu.SemaphoreType.DMA((5,)),
         pltpu.SemaphoreType.DMA((MESSAGES,)),
         pltpu.SemaphoreType.DMA((MESSAGES,)),
     ]
     anywhere = pl.BlockSpec(memory_space=pl.ANY)
     inside = pl.BlockSpec(memory_space=vmem)
-    out = pl.pallas_call(
+    mix, slot_rows = pl.pallas_call(
         kernel,
-        out_shape=jax.ShapeDtypeStruct((count, width), BF16),
+        out_shape=[
+            jax.ShapeDtypeStruct((RING, rows, slots), BF16),
+            jax.ShapeDtypeStruct((RING, 8, 16, width), BF16),
+        ],
         in_specs=[anywhere, inside, anywhere, anywhere, anywhere, anywhere],
-        out_specs=inside,
+        out_specs=[inside, inside],
         scratch_shapes=scratch,
         compiler_params=pltpu.CompilerParams(
             collective_id=0, has_side_effects=True, vmem_limit_bytes=60 << 20
         ),
         name="soft_moe",
-    )(tokens[0], gain[None], phi, w_gate[0], w_up[0], w_down[0])
-    return out[None]
+    )(tokens[0], gain.reshape(-1, 128), phi, w_gate[0], w_up[0], w_down[0])
+    out = jnp.dot(
+        mix.reshape(count, slots), slot_rows.reshape(slots, width), preferred_element_type=F32
+    )
+    return out.astype(BF16)[None]
 
 
 def solution(mesh):

time: 124 us -> 110 us (0.89); the launches traced: 122 us -> 110 us
  Pallas kernels: 119 us -> 107 us
  local copies, waits for them, and re-layouts: 3.15 us -> 0 us
  matrix products: 0 us -> 2.55 us
    pallas_call x1, Pallas kernels: 119 us -> 107 us  [local(): pl.pallas_call(kernel, out_shape=[jax.ShapeDtypeStruct((RING, rows, slots...]
    dot_general x0 -> x1, matrix products: none -> 2.55 us  [local(): jnp.dot(mix.reshape(count, slots), slot_rows.reshape(slots, width), prefe...]
    unnamed x1 -> x0, local copies, waits for them, and re-layouts: 1.87 us -> none
    broadcast_in_dim x1 -> x0, local copies, waits for them, and re-layouts: 1.28 us -> none  [local(): gain[None]]
where the time goes in v2:
time: 110 us
  Pallas kernels  107 us (97%)
  matrix products  2.55 us (2%)
    pallas_call x1, Pallas kernels, local(): pl.pallas_call(kernel, out_shape=[jax.ShapeDtypeStruct((RING, rows, slots...  107 us
    dot_general x1, matrix products, local(): jnp.dot(mix.reshape(count, slots), slot_rows.reshape(slots, width), prefe...  2.55 us

profile of v2, /device:TPU:0, one launch (start us, length us, event | category | flops | bytes accessed | tf_op | source)
XLA Modules:
  0.0 110.0 jit_solution(5125706970083551003)
XLA Ops:
  0.0 107.5 %soft_moe.1 = (bf16[4,64,512]{2,1,0:T(8,128)(2,1)}, bf16[4,8,16,1024]{3,2,1,0:T(8,128)(2,1)}) custom-call(bf16[256,1024]{1,0:T(8,128)(2,1)} %bitcast.15, bf16[8,128]{1,0:T(8,128)(2,1)} %bitcast.17, bf16[1024,512]{1,0:T(8,128)(2,1)} %phi_in.1, bf16[4096,896]{1,0:T(8,128)(2,1)} %bitcast.11, bf16[4096,896]{1,0:T(8,128)(2,1)} %bitcast.12, bf16[896,4096]{1,0:T(8,128)(2,1)} %bitcast.13), custom_call_target="tpu_custom_call" | custom-call | tf_op jit(solution)/shard_map/soft_moe/pallas_call | solution.py:563
  107.5 2.5 %fusion = bf16[1,256,1024]{2,1,0:T(8,128)(2,1)} fusion(bf16[256,512]{1,0:T(8,128)(2,1)} %bitcast.16, bf16[512,1024]{1,0:T(8,128)(2,1)} %bitcast.14), kind=kOutput, calls=%fused_computation.1 | convolution fusion | flops 268697600 | bytes 1835008 | tf_op jit(solution)/shard_map/dot_general | solution.py:577

commit v3 on v2

--- a/solution.py
+++ b/solution.py
@@ -10,6 +10,10 @@
 RING = 4
 BF16 = jnp.bfloat16
 F32 = jnp.float32
+
+
+def keep(v):
+    return pltpu.with_memory_space_constraint(v, pltpu.HBM)
 
 
 def near(v):
@@ -127,7 +131,7 @@
 
     barrier = pltpu.get_barrier_semaphore()
     plane = [(dy, dz) for dy in range(RING) for dz in range(RING) if (dy, dz) != (0, 0)]
-    across = [(dx, dc) for dx in (2, 1, 3, 0) for dc in range(2) if (dx, dc) != (0, 0)]
+    across = [(dx, dc) for dx in (0, 1, 3, 2) for dc in range(2) if (dx, dc) != (0, 0)]
 
     def in_plane(dy, dz):
         return {"batch": near(y + dy), "tensor": near(z + dz)}
@@ -229,6 +233,14 @@
     for k in (1, 0, 2):
         to = near(y + k + 1)
         net.start(first_q + k, qo.at[to], qg.at[z, y], {"batch": to})
+    first_qz = net.take(12)
+
+    def spread(k):
+        block = qg.at[z, near(y - k)]
+        for n in (0, 2, 1):
+            net.start(first_qz + 3 * k + n, block, block, {"tensor": near(z + n + 1)})
+
+    spread(0)
     first_st = net.take(len(plane))
     for k, step in enumerate(plane):
         net.start(first_st + k, mine, mine, in_plane(*step))
@@ -239,14 +251,18 @@
     row_max = jnp.max(logits, axis=1, keepdims=True)
     row_raised = jnp.exp(logits - row_max)
     cb[z] = (row_raised / jnp.sum(row_raised, axis=1, keepdims=True)).astype(BF16)
-    for k in range(3):
-        net.arrived(first_q + k, qg.at[z, near(y - k - 1)], {"batch": near(y + k + 1)})
-    q_pieces = [
-        Gather(net, "tensor", z, d, lambda b, i=i: qg.at[b, pl.ds(i * 2, 2)])
+    mix_pieces = [
+        Gather(net, "tensor", z, d, lambda b, i=i: cb.at[b, pl.ds(i * half, half)])
         for i, d in enumerate((1, -1))
     ]
-    for piece in q_pieces:
+    for piece in mix_pieces:
         piece.start()
+    for k in (1, 3, 2):
+        net.arrived(first_q + k - 1, qg.at[z, near(y - k)], {"batch": near(y + k)})
+        spread(k)
+        if k == 3:
+            token_pieces[2].relay()
+    token_pieces[3].relay()
     for k, (dy, dz) in enumerate(plane):
         net.arrived(first_st + k, st.at[near(y - dy), near(z - dz)], in_plane(dy, dz))
     maxima = st[:, :, pl.ds(y, 1), :]
@@ -255,18 +271,15 @@
     weights = jnp.exp(maxima - top)
     total = jnp.sum(jnp.sum(totals * weights, axis=1, keepdims=True), axis=0, keepdims=True)
     weights = weights / total
-    for piece in q_pieces:
+    for piece in mix_pieces:
         piece.relay()
-    token_pieces[2].relay()
-    token_pieces[3].relay()
-    mix_pieces = [
-        Gather(net, "tensor", z, d, lambda b, i=i: cb.at[b, pl.ds(i * half, half)])
-        for i, d in enumerate((1, -1))
-    ]
-    for piece in q_pieces:
-        piece.direct()
-    for piece in q_pieces:
-        piece.last()
+    for k in (0, 1, 3, 2):
+        for n in range(3):
+            net.arrived(
+                first_qz + 3 * k + n,
+                qg.at[near(z - n - 1), near(y - k)],
+                {"tensor": near(z + n + 1)},
+            )
     for b in range(RING):
         scaled_q = jnp.concatenate(
             [qg[k, b].astype(F32) * weights[b, k] for k in range(RING)], axis=0
@@ -276,8 +289,6 @@
         piece.direct()
     for piece in token_pieces:
         piece.last()
-    for piece in mix_pieces:
-        piece.start()
 
     tile = 256
     for j in range(width // tile):
@@ -288,7 +299,7 @@
         si[:, :, at] = part.astype(BF16).reshape(8, 16, tile)
 
     def place(k, core):
-        return xs.at[z, k // 2, y, pl.ds(lax.rem(k, 2) * 32 + core * 16, 16)]
+        return xs.at[z, k % 2, y, pl.ds(k // 2 * 32 + core * 16, 16)]
 
     first_x = net.take(len(across))
     for n, (dx, dc) in enumerate(across):
@@ -322,14 +333,14 @@
         for j, d in zip(steps, ways)
     ]
 
-    for k in (0, 1):
-        wait_x(k)
-        a1[k].start()
-    for k in (2, 3):
-        wait_x(k)
-        b1[k - 2].start()
-    for piece in mix_pieces:
-        piece.relay()
+    wait_x(0)
+    a1[0].start()
+    wait_x(1)
+    b1[0].start()
+    wait_x(3)
+    b1[1].start()
+    wait_x(2)
+    a1[1].start()
     a2[0].start()
     b2[0].start()
     for stage in (a1, b1):
@@ -340,66 +351,66 @@
             piece.direct()
         later[1].start()
         later[2].start()
-    for stage, later in ((a1, a2), (b1, b2)):
-        for piece in stage:
-            piece.last()
-        later[3].start()
+    for piece in a1:
+        piece.last()
+    a2[3].start()
+    for piece in b1:
+        piece.last()
+    b2[0].relay()
+    b2[3].start()
 
     loads[2].wait()
     loads[3].wait()
     share = acc.shape[0]
 
-    def raise_rows(b, halves, first=False, last=False):
+    def raise_rows(h, b, first=False, last=False):
         deep = pl.ds(pl.multiple_of(b * width, width), width)
-        lo, hi = halves[0], halves[-1] + 1
-        count = (hi - lo) * RING * 64
-        block = xs[b, lo:hi].reshape(count, width)
+        block = xs[b, h].reshape(RING * 64, width)
         for j in range(share):
             at = pl.ds(j * 128, 128)
             both = jnp.concatenate([wg[deep, at], wu[deep, at]], axis=1)
             part = jnp.dot(block, both, preferred_element_type=F32)
             if not first:
-                part = acc[j, lo:hi].reshape(count, 256) + part
+                part = acc[j, h] + part
             if last:
                 gate, up = part[:, :128], part[:, 128:]
-                hid[:, at] = (gate / (1.0 + jnp.exp(-gate)) * up).astype(BF16)
+                hid[h, :, at] = (gate / (1.0 + jnp.exp(-gate)) * up).astype(BF16)
             else:
-                acc[j, lo:hi] = part.reshape(hi - lo, RING * 64, 256)
-
-    raise_rows(z, (0,), first=True)
+                acc[j, h] = part
+
+    raise_rows(0, z, first=True)
     a2[0].relay()
-    b2[0].relay()
+    b2[1].relay()
+    a2[1].relay()
+    b2[2].relay()
     a2[2].relay()
-    b2[2].relay()
     b2[0].direct()
-    a2[1].relay()
-    b2[1].relay()
     b2[0].last()
-    raise_rows(z, (1,), first=True)
-    a2[3].relay()
-    b2[3].relay()
+    raise_rows(1, z, first=True)
     for piece in a2:
         piece.direct()
+    raise_rows(0, near(z - 1))
+    b2[3].relay()
+    a2[3].relay()
+    raise_rows(0, near(z + 1))
+    b2[2].direct()
+    b2[2].last()
+    raise_rows(1, near(z + 1))
     b2[1].direct()
     b2[1].last()
-    raise_rows(near(z - 1), (0, 1))
-    b2[2].direct()
-    b2[2].last()
-    raise_rows(near(z + 1), (0, 1))
+    raise_rows(1, near(z - 1))
     for piece in a2:
         piece.last()
-    b2[3].direct()
-    b2[3].last()
-    raise_rows(near(z + 2), (0, 1), last=True)
+    raise_rows(0, near(z + 2), last=True)
 
     loads[4].wait()
 
-    def lower_rows(b):
+    def lower_rows(h, b):
         for j in range(width // tile):
             inside = pl.ds(j * tile, tile)
             at = pl.ds(pl.multiple_of(b * width + j * tile, tile), tile)
-            part = jnp.dot(hid[...], wd[:, at], preferred_element_type=F32)
-            ys[b, :, :, :, inside] = part.astype(BF16).reshape(2, RING, 64, tile)
+            part = jnp.dot(hid[h], wd[:, at], preferred_element_type=F32)
+            ys[b, h, :, :, inside] = part.astype(BF16).reshape(RING, 64, tile)
 
     order = (2, 1, 3, 0)
     sides = (1, -1, 1, -1)
@@ -436,55 +447,61 @@
         for i, d in enumerate((1, -1))
     ]
 
-    lower_rows(near(z + 2))
+    lower_rows(0, near(z + 2))
     for piece in ra1:
         piece.send_far()
+    b2[3].direct()
+    b2[3].last()
+    raise_rows(1, near(z + 2), last=True)
+    lower_rows(1, near(z + 2))
     rb1[0].send_far()
     rb1[0].send_near()
-    lower_rows(near(z + 1))
+    lower_rows(1, near(z + 1))
+    rb1[1].send_far()
+    rb1[1].send_near()
+    lower_rows(0, near(z + 1))
     ra1[1].send_near()
     ra1[3].send_near()
-    rb1[1].send_far()
-    rb1[1].send_near()
-    lower_rows(near(z - 1))
+    lower_rows(0, near(z - 1))
     ra1[0].send_near()
     ra1[2].send_near()
+    lower_rows(1, near(z - 1))
     rb1[2].send_far()
     rb1[2].send_near()
-    lower_rows(z)
+    ra1[0].relay()
+    ra1[1].relay()
+    lower_rows(1, z)
     rb1[3].send_far()
     rb1[3].send_near()
-    ra1[0].relay()
-    ra1[1].relay()
     rb1[0].relay()
-    rb1[1].relay()
+    lower_rows(0, z)
     ra1[2].relay()
     ra1[3].relay()
+    rb1[1].relay()
     rb1[2].relay()
     rb1[3].relay()
 
     def close_sum(pieces, n, sums, me):
         sums[near(me + order[n])] = pieces[n].finish().astype(BF16)
 
-    close_sum(ra1, 0, a_sum, y)
-    for piece in ra2:
-        piece.send_far()
-    close_sum(rb1, 0, b_sum, z)
-    for piece in rb2:
-        piece.send_far()
-    for n in (1, 2):
-        close_sum(ra1, n, a_sum, y)
-        close_sum(rb1, n, b_sum, z)
-    for piece in (*ra2, *rb2):
-        piece.send_near()
-    for piece in (*ra2, *rb2):
-        piece.relay()
-    close_sum(ra1, 3, a_sum, y)
-    close_sum(rb1, 3, b_sum, z)
+    both = ((ra1, a_sum, y, ra2), (rb1, b_sum, z, rb2))
+    for stage, sums, me, later in both:
+        close_sum(stage, 0, sums, me)
+        later[0].send_far()
+        later[1].send_far()
+        close_sum(stage, 1, sums, me)
+        later[1].send_near()
+    for stage, sums, me, later in both:
+        later[0].relay()
+        close_sum(stage, 2, sums, me)
+        later[0].send_near()
+        later[1].relay()
+    for stage, sums, me, later in both:
+        close_sum(stage, 3, sums, me)
 
     first_back = net.take(len(across))
     backs = {step: first_back + n for n, step in enumerate(across)}
-    for k, piece in enumerate((*ra2, *rb2)):
+    for k, piece in ((1, rb2[0]), (3, rb2[1]), (2, ra2[1]), (0, ra2[0])):
         so[k] = piece.finish().astype(BF16)
         for dc in range(2):
             core = lax.rem(c + dc, 2)
@@ -498,12 +515,12 @@
         Gather(net, "batch", y, d, lambda b, k=k: rf.at[b, pl.ds(2 * near(x - k), 2)])
         for k, d in enumerate((1, -1, 1, -1))
     ]
-    for k, piece in enumerate(out_pieces):
+    for k in (0, 1, 3, 2):
         for dc in range(2):
             if (k, dc) != (0, 0):
                 source = near(x - k) * 2 + lax.rem(c + dc, 2)
                 net.arrived(backs[k, dc], rf.at[y, source], over_x(k, dc))
-        piece.start()
+        out_pieces[k].start()
     for piece in out_pieces:
         piece.relay()
     for piece in out_pieces:
@@ -517,7 +534,7 @@
     net.drain()
 
 
-MESSAGES = 149
+MESSAGES = 155
 
 
 def local(tokens, gain, phi, w_gate, w_up, w_down):
@@ -545,7 +562,7 @@
         vmem((8, 16, width), BF16),
         vmem((RING, 2, RING, 64, width), BF16),
         vmem((share // 128, 2, 256, 256), F32),
-        vmem((512, share), BF16),
+        vmem((2, 256, share), BF16),
         vmem((RING, 2, RING, 64, width), BF16),
         vmem((3, 4, 64, width), BF16),
         vmem((RING, 64, width), BF16),
@@ -558,7 +575,7 @@
         pltpu.SemaphoreType.DMA((MESSAGES,)),
         pltpu.SemaphoreType.DMA((MESSAGES,)),
     ]
-    anywhere = pl.BlockSpec(memory_space=pl.ANY)
+    anywhere = pl.BlockSpec(memory_space=pltpu.HBM)
     inside = pl.BlockSpec(memory_space=vmem)
     mix, slot_rows = pl.pallas_call(
         kernel,
@@ -570,10 +587,10 @@
         out_specs=[inside, inside],
         scratch_shapes=scratch,
         compiler_params=pltpu.CompilerParams(
-            collective_id=0, has_side_effects=True, vmem_limit_bytes=60 << 20
+            collective_id=0, has_side_effects=True, vmem_limit_bytes=48 << 20
         ),
         name="soft_moe",
-    )(tokens[0], gain.reshape(-1, 128), phi, w_gate[0], w_up[0], w_down[0])
+    )(keep(tokens[0]), keep(gain.reshape(-1, 128)), keep(phi), w_gate[0], w_up[0], w_down[0])
     out = jnp.dot(
         mix.reshape(count, slots), slot_rows.reshape(slots, width), preferred_element_type=F32
     )

time: 110 us -> 104 us (0.945)
  Pallas kernels: 107 us -> 103 us
  matrix products: 2.55 us -> 1.24 us
    pallas_call x1, Pallas kernels: 107 us -> 103 us  [local(): pl.pallas_call(kernel, out_shape=[jax.ShapeDtypeStruct((RING, rows, slots...]
    dot_general x1, matrix products: 2.55 us -> 1.24 us  [local(): jnp.dot(mix.reshape(count, slots), slot_rows.reshape(slots, width), prefe...]
where the time goes in v3:
time: 104 us
  Pallas kernels  103 us (99%)
  matrix products  1.24 us (1%)
    pallas_call x1, Pallas kernels, local(): pl.pallas_call(kernel, out_shape=[jax.ShapeDtypeStruct((RING, rows, slots...  103 us

profile of v3, /device:TPU:0, one launch (start us, length us, event | category | flops | bytes accessed | tf_op | source)
XLA Modules:
  0.0 103.8 jit_solution(8408647283682817568)
XLA Ops:
  0.0 102.5 %soft_moe.1 = (bf16[4,64,512]{2,1,0:T(8,128)(2,1)S(1)}, bf16[4,8,16,1024]{3,2,1,0:T(8,128)(2,1)S(1)}) custom-call(bf16[256,1024]{1,0:T(8,128)(2,1)} %bitcast.16, bf16[8,128]{1,0:T(8,128)(2,1)} %bitcast.17, bf16[1024,512]{1,0:T(8,128)(2,1)} %phi_in.1, bf16[4096,896]{1,0:T(8,128)(2,1)} %bitcast.13, bf16[4096,896]{1,0:T(8,128)(2,1)} %bitcast.14, ...), custom_call_target="tpu_custom_call" | custom-call | tf_op jit(solution)/shard_map/soft_moe/pallas_call | solution.py:580
  102.5 1.2 %fusion = bf16[1,256,1024]{2,1,0:T(8,128)(2,1)} fusion(bf16[256,512]{1,0:T(8,128)(2,1)S(1)} %bitcast.12, bf16[512,1024]{1,0:T(8,128)(2,1)S(1)} %bitcast.11), kind=kOutput, calls=%fused_computation.1 | convolution fusion | flops 268697600 | bytes 1835008 | tf_op jit(solution)/shard_map/dot_general | solution.py:594

commit v4 on v3

--- a/solution.py
+++ b/solution.py
@@ -154,6 +154,34 @@
     tokens_f = tok[...].astype(F32)
     scaled = (tokens_f * wide.astype(F32)).astype(BF16)
     tg[y] = scaled
+    loads[1].wait()
+    part = jnp.dot(scaled, phi[...], preferred_element_type=F32)
+    lp[...] = part.reshape(lp.shape)
+    for one in loads[2:]:
+        one.start()
+
+    pl.semaphore_wait(barrier, len(peers))
+
+    half = rows // 2
+    logit_pieces = [
+        Scatter(
+            net, "tensor", z, d,
+            lambda b, i=i: lp.at[b, pl.ds(i * 16, 16)],
+            [l_in.at[k, i] for k in range(3)],
+        )
+        for i, d in enumerate((1, -1, 1, -1))
+    ]
+    token_pieces = [
+        Gather(net, "batch", y, d, lambda b, i=i: tg.at[b, :, pl.ds(i * 256, 256)])
+        for i, d in enumerate((1, -1, 1, -1))
+    ]
+    for piece in logit_pieces:
+        piece.send_far()
+    for piece in logit_pieces:
+        piece.send_near()
+    token_pieces[0].start()
+    token_pieces[1].start()
+
     squares = jnp.sum(tokens_f * tokens_f, axis=1, keepdims=True)
     diagonal = lax.broadcasted_iota(jnp.int32, (rows, 128), 0) == lax.broadcasted_iota(
         jnp.int32, (rows, 128), 1
@@ -162,40 +190,10 @@
         column = squares[b * rows : (b + 1) * rows]
         line = jnp.sum(jnp.where(diagonal, column, 0.0), axis=0, keepdims=True)
         sq_out[b] = jnp.broadcast_to(line, (8, 128))
-    loads[1].wait()
-    for b in range(RING):
-        part = jnp.dot(
-            scaled[b * rows : (b + 1) * rows, :], phi[...], preferred_element_type=F32
-        )
-        lp[b] = part
-    for one in loads[2:]:
-        one.start()
-
-    pl.semaphore_wait(barrier, len(peers))
-
-    half = rows // 2
-    logit_pieces = [
-        Scatter(
-            net, "tensor", z, d,
-            lambda b, i=i: lp.at[b, pl.ds(i * half, half)],
-            [l_in.at[k, i] for k in range(3)],
-        )
-        for i, d in enumerate((1, -1))
-    ]
-    token_pieces = [
-        Gather(net, "batch", y, d, lambda b, i=i: tg.at[b, pl.ds(i * rows, rows)])
-        for i, d in enumerate((1, -1, 1, -1))
-    ]
-    for piece in logit_pieces:
-        piece.send_far()
     first_sq = net.take(3)
     for k in range(3):
         to = near(z + k + 1)
         net.start(first_sq + k, sq_out.at[to], sq_in.at[k], {"tensor": to})
-    for piece in logit_pieces:
-        piece.send_near()
-    token_pieces[0].start()
-    token_pieces[1].start()
     for piece in logit_pieces:
         piece.relay()
     token_pieces[2].start()
@@ -285,34 +283,43 @@
             [qg[k, b].astype(F32) * weights[b, k] for k in range(RING)], axis=0
         )
         qt[:, b * RING * rows : (b + 1) * RING * rows] = scaled_q.T.astype(BF16)
-    for piece in token_pieces:
-        piece.direct()
-    for piece in token_pieces:
-        piece.last()
-
     tile = 256
-    for j in range(width // tile):
-        at = pl.ds(j * tile, tile)
-        part = jnp.dot(
-            qt[...], tg[:, :, at].reshape(qt.shape[1], tile), preferred_element_type=F32
-        )
-        si[:, :, at] = part.astype(BF16).reshape(8, 16, tile)
-
-    def place(k, core):
-        return xs.at[z, k % 2, y, pl.ds(k // 2 * 32 + core * 16, 16)]
-
-    first_x = net.take(len(across))
-    for n, (dx, dc) in enumerate(across):
-        target = over_x(dx, dc)
-        net.start(
-            first_x + n, si.at[target["expert"]], place((RING - dx) % RING, c), target
-        )
-    place(0, c)[...] = si[e]
+
+    def place(k, core, part):
+        inside = pl.ds(k // 2 * 32 + core * 16, 16)
+        return xs.at[z, k % 2, y, inside, pl.ds(part * 2 * tile, 2 * tile)]
+
+    first_x = net.take(2 * len(across))
+    for part in range(2):
+        for piece in token_pieces[2 * part : 2 * part + 2]:
+            piece.direct()
+            piece.last()
+        for j in (2 * part, 2 * part + 1):
+            at = pl.ds(j * tile, tile)
+            made = jnp.dot(
+                qt[...], tg[:, :, at].reshape(qt.shape[1], tile), preferred_element_type=F32
+            )
+            si[:, :, at] = made.astype(BF16).reshape(8, 16, tile)
+        own = pl.ds(part * 2 * tile, 2 * tile)
+        for n, (dx, dc) in enumerate(across):
+            target = over_x(dx, dc)
+            net.start(
+                first_x + 2 * n + part,
+                si.at[target["expert"], :, own],
+                place((RING - dx) % RING, c, part),
+                target,
+            )
+        place(0, c, part)[...] = si[e, :, own]
 
     def wait_x(k):
         for n, (dx, dc) in enumerate(across):
             if (RING - dx) % RING == k:
-                net.arrived(first_x + n, place(k, lax.rem(c + dc, 2)), over_x(dx, dc))
+                for part in range(2):
+                    net.arrived(
+                        first_x + 2 * n + part,
+                        place(k, lax.rem(c + dc, 2), part),
+                        over_x(dx, dc),
+                    )
 
     a1 = [
         Gather(net, "batch", y, d, lambda b, i=i: xs.at[z, 0, b, pl.ds(i * 32, 32)])
@@ -430,21 +437,26 @@
         )
         for i, (j, d) in enumerate(zip(order, sides))
     ]
+    minor = [(kk, dc) for kk in range(2) for dc in range(2)]
+
+    def strip(kk, dc):
+        return pl.ds(kk * 32 + lax.rem(c + dc, 2) * 16, 16)
+
     ra2 = [
         Scatter(
-            net, "batch", y, d,
-            lambda b, i=i: a_sum.at[b, pl.ds(i * 32, 32)],
-            [a2_in.at[k, i] for k in range(3)],
-        )
-        for i, d in enumerate((1, -1))
+            net, "batch", y, 1 - 2 * dc,
+            lambda b, kk=kk, dc=dc: a_sum.at[b, strip(kk, dc)],
+            [a2_in.at[k, 2 * kk + dc] for k in range(3)],
+        )
+        for kk, dc in minor
     ]
     rb2 = [
         Scatter(
-            net, "tensor", z, d,
-            lambda b, i=i: b_sum.at[b, pl.ds(i * 32, 32)],
-            [b2_in.at[k, i] for k in range(3)],
-        )
-        for i, d in enumerate((1, -1))
+            net, "tensor", z, 1 - 2 * dc,
+            lambda b, kk=kk, dc=dc: b_sum.at[b, strip(kk, dc)],
+            [b2_in.at[k, 2 * kk + dc] for k in range(3)],
+        )
+        for kk, dc in minor
     ]
 
     lower_rows(0, near(z + 2))
@@ -484,48 +496,68 @@
     def close_sum(pieces, n, sums, me):
         sums[near(me + order[n])] = pieces[n].finish().astype(BF16)
 
-    both = ((ra1, a_sum, y, ra2), (rb1, b_sum, z, rb2))
-    for stage, sums, me, later in both:
+    both = (
+        (ra1, a_sum, y, (ra2[2], ra2[0]), (ra2[3], ra2[1])),
+        (rb1, b_sum, z, (rb2[0], rb2[2]), (rb2[1], rb2[3])),
+    )
+    for stage, sums, me, plus, minus in both:
         close_sum(stage, 0, sums, me)
-        later[0].send_far()
-        later[1].send_far()
+        for piece in (*plus, *minus):
+            piece.send_far()
         close_sum(stage, 1, sums, me)
-        later[1].send_near()
-    for stage, sums, me, later in both:
-        later[0].relay()
+        for piece in minus:
+            piece.send_near()
+    for stage, sums, me, plus, minus in both:
+        for piece in plus:
+            piece.relay()
         close_sum(stage, 2, sums, me)
-        later[0].send_near()
-        later[1].relay()
-    for stage, sums, me, later in both:
+        for piece in plus:
+            piece.send_near()
+        for piece in minus:
+            piece.relay()
+    for stage, sums, me, plus, minus in both:
         close_sum(stage, 3, sums, me)
 
     first_back = net.take(len(across))
     backs = {step: first_back + n for n, step in enumerate(across)}
-    for k, piece in ((1, rb2[0]), (3, rb2[1]), (2, ra2[1]), (0, ra2[0])):
-        so[k] = piece.finish().astype(BF16)
+    for k, stage in ((1, rb2), (2, ra2), (3, rb2), (0, ra2)):
         for dc in range(2):
-            core = lax.rem(c + dc, 2)
-            mine = so.at[k, pl.ds(core * 16, 16)]
+            done = stage[k // 2 * 2 + dc].finish().astype(BF16)
             if (k, dc) == (0, 0):
-                rf[y, e] = mine[...]
+                rf[y, e] = done
             else:
-                net.start(backs[k, dc], mine, rf.at[y, e], over_x(k, dc))
-
-    out_pieces = [
-        Gather(net, "batch", y, d, lambda b, k=k: rf.at[b, pl.ds(2 * near(x - k), 2)])
-        for k, d in enumerate((1, -1, 1, -1))
-    ]
-    for k in (0, 1, 3, 2):
+                so[k, dc] = done
+                net.start(backs[k, dc], so.at[k, dc], rf.at[y, e], over_x(k, dc))
+
+    def source(k, dc):
+        return near(x - k) * 2 + lax.rem(c + dc, 2)
+
+    out_pieces = {
+        (k, dc): Gather(
+            net, "batch", y, 1 - 2 * dc, lambda b, k=k, dc=dc: rf.at[b, source(k, dc)]
+        )
+        for k in range(RING)
+        for dc in range(2)
+    }
+
+    def start_out(k):
         for dc in range(2):
             if (k, dc) != (0, 0):
-                source = near(x - k) * 2 + lax.rem(c + dc, 2)
-                net.arrived(backs[k, dc], rf.at[y, source], over_x(k, dc))
-        out_pieces[k].start()
-    for piece in out_pieces:
-        piece.relay()
-    for piece in out_pieces:
+                net.arrived(backs[k, dc], rf.at[y, source(k, dc)], over_x(k, dc))
+            out_pieces[k, dc].start()
+
+    start_out(0)
+    start_out(1)
+    start_out(3)
+    for dc in range(2):
+        out_pieces[0, dc].relay()
+    start_out(2)
+    for k in (1, 3, 2):
+        for dc in range(2):
+            out_pieces[k, dc].relay()
+    for piece in out_pieces.values():
         piece.direct()
-    for piece in out_pieces:
+    for piece in out_pieces.values():
         piece.last()
 
     for piece in mix_pieces:
@@ -534,7 +566,7 @@
     net.drain()
 
 
-MESSAGES = 155
+MESSAGES = 192
 
 
 def local(tokens, gain, phi, w_gate, w_up, w_down):
@@ -552,7 +584,7 @@
         vmem((share, D), BF16),
         vmem((RING, count, width), BF16),
         vmem((RING, rows, slots), F32),
-        vmem((3, 2, rows // 2, slots), F32),
+        vmem((3, 4, 16, slots), F32),
         vmem((RING, 8, 128), F32),
         vmem((3, 8, 128), F32),
         vmem((RING, RING, 8, 128), F32),
@@ -566,11 +598,11 @@
         vmem((RING, 2, RING, 64, width), BF16),
         vmem((3, 4, 64, width), BF16),
         vmem((RING, 64, width), BF16),
-        vmem((3, 2, 32, width), BF16),
+        vmem((3, 4, 16, width), BF16),
         vmem((3, 4, 64, width), BF16),
         vmem((RING, 64, width), BF16),
-        vmem((3, 2, 32, width), BF16),
-        vmem((4, 32, width), BF16),
+        vmem((3, 4, 16, width), BF16),
+        vmem((4, 2, 16, width), BF16),
         pltpu.SemaphoreType.DMA((5,)),
         pltpu.SemaphoreType.DMA((MESSAGES,)),
         pltpu.SemaphoreType.DMA((MESSAGES,)),

time: 104 us -> 103 us (level)
  no operation moved by 1% of the time
where the time goes in v4:
time: 103 us
  Pallas kernels  102 us (99%)
  matrix products  1.24 us (1%)
    pallas_call x1, Pallas kernels, local(): pl.pallas_call(kernel, out_shape=[jax.ShapeDtypeStruct((RING, rows, slots...  102 us

profile of v4, /device:TPU:0, one launch (start us, length us, event | category | flops | bytes accessed | tf_op | source)
XLA Modules:
  0.0 103.2 jit_solution(10806531869017457912)
XLA Ops:
  0.0 101.9 %soft_moe.1 = (bf16[4,64,512]{2,1,0:T(8,128)(2,1)S(1)}, bf16[4,8,16,1024]{3,2,1,0:T(8,128)(2,1)S(1)}) custom-call(bf16[256,1024]{1,0:T(8,128)(2,1)} %bitcast.16, bf16[8,128]{1,0:T(8,128)(2,1)} %bitcast.17, bf16[1024,512]{1,0:T(8,128)(2,1)} %phi_in.1, bf16[4096,896]{1,0:T(8,128)(2,1)} %bitcast.13, bf16[4096,896]{1,0:T(8,128)(2,1)} %bitcast.14, ...), custom_call_target="tpu_custom_call" | custom-call | tf_op jit(solution)/shard_map/soft_moe/pallas_call | solution.py:612
  101.9 1.2 %fusion = bf16[1,256,1024]{2,1,0:T(8,128)(2,1)} fusion(bf16[256,512]{1,0:T(8,128)(2,1)S(1)} %bitcast.12, bf16[512,1024]{1,0:T(8,128)(2,1)S(1)} %bitcast.11), kind=kOutput, calls=%fused_computation.1 | convolution fusion | flops 268697600 | bytes 1835008 | tf_op jit(solution)/shard_map/dot_general | solution.py:626

commit v5 on v4

--- a/solution.py
+++ b/solution.py
@@ -23,9 +23,9 @@
 class Net:
     def __init__(self, send_sems, recv_sems):
         self.send_sems, self.recv_sems = send_sems, recv_sems
-        self.used, self.sent = 0, []
-
-    def take(self, count=1):
+        self.used, self.count, self.sent = 0, 0, {}
+
+    def take(self, count):
         first = self.used
         self.used += count
         return first
@@ -34,22 +34,26 @@
         return pltpu.make_async_remote_copy(
             src_ref=src,
             dst_ref=dst,
-            send_sem=self.send_sems.at[n],
+            send_sem=self.send_sems.at[self.count % SENDS],
             recv_sem=self.recv_sems.at[n],
             device_id=target,
             device_id_type=pl.DeviceIdType.MESH,
         )
 
     def start(self, n, src, dst, target):
+        slot = self.count % SENDS
+        if slot in self.sent:
+            self.sent[slot].wait_send()
         one = self.copy(n, src, dst, target)
         one.start()
-        self.sent.append(one)
+        self.sent[slot] = one
+        self.count += 1
 
     def arrived(self, n, dst, target):
         self.copy(n, dst, dst, target).wait_recv()
 
     def drain(self):
-        for one in self.sent:
+        for one in self.sent.values():
             one.wait_send()
 
 
@@ -321,6 +325,7 @@
                         over_x(dx, dc),
                     )
 
+    fresh, net.used = net.used, 0
     a1 = [
         Gather(net, "batch", y, d, lambda b, i=i: xs.at[z, 0, b, pl.ds(i * 32, 32)])
         for i, d in enumerate((1, -1))
@@ -329,42 +334,48 @@
         Gather(net, "tensor", z, d, lambda b, i=i: xs.at[b, 1, y, pl.ds(i * 32, 32)])
         for i, d in enumerate((1, -1))
     ]
-    steps = (0, 3, 1, 2)
-    ways = (1, 1, -1, -1)
+    net.used = fresh
+    low, high, whole = pl.ds(0, 32), pl.ds(32, 32), pl.ds(0, 64)
+    cuts = ((0, low, 1), (0, high, -1), (3, whole, 1), (1, whole, -1), (2, low, 1), (2, high, -1))
     a2 = [
-        Gather(net, "tensor", z, d, lambda b, j=j: xs.at[b, 0, near(y + j)])
-        for j, d in zip(steps, ways)
+        Gather(net, "tensor", z, d, lambda b, j=j, r=r: xs.at[b, 0, near(y + j), r])
+        for j, r, d in cuts
     ]
     b2 = [
-        Gather(net, "batch", y, d, lambda b, j=j: xs.at[near(z + j), 1, b])
-        for j, d in zip(steps, ways)
+        Gather(net, "batch", y, d, lambda b, j=j, r=r: xs.at[near(z + j), 1, b, r])
+        for j, r, d in cuts
     ]
 
     wait_x(0)
     a1[0].start()
+    a2[0].start()
     wait_x(1)
     b1[0].start()
+    b2[0].start()
     wait_x(3)
     b1[1].start()
     wait_x(2)
     a1[1].start()
-    a2[0].start()
-    b2[0].start()
-    for stage in (a1, b1):
-        for piece in stage:
-            piece.relay()
+    b2[1].start()
+    a2[1].start()
+    for piece in (*a1, *b1):
+        piece.relay()
     for stage, later in ((a1, a2), (b1, b2)):
         for piece in stage:
             piece.direct()
-        later[1].start()
         later[2].start()
-    for piece in a1:
+        later[3].start()
+    for i in range(2):
+        a1[i].last()
+        a2[4 + i].start()
+    b2[0].relay()
+    b2[1].relay()
+    for i in range(2):
+        b1[i].last()
+        b2[4 + i].start()
+    for piece in mix_pieces:
+        piece.direct()
         piece.last()
-    a2[3].start()
-    for piece in b1:
-        piece.last()
-    b2[0].relay()
-    b2[3].start()
 
     loads[2].wait()
     loads[3].wait()
@@ -387,24 +398,28 @@
 
     raise_rows(0, z, first=True)
     a2[0].relay()
-    b2[1].relay()
     a2[1].relay()
     b2[2].relay()
     a2[2].relay()
-    b2[0].direct()
-    b2[0].last()
+    b2[3].relay()
+    a2[3].relay()
+    for piece in b2[:2]:
+        piece.direct()
+        piece.last()
     raise_rows(1, z, first=True)
     for piece in a2:
         piece.direct()
+    a2[4].relay()
+    a2[5].relay()
     raise_rows(0, near(z - 1))
-    b2[3].relay()
-    a2[3].relay()
+    b2[4].relay()
+    b2[5].relay()
     raise_rows(0, near(z + 1))
+    b2[3].direct()
+    b2[3].last()
+    raise_rows(1, near(z + 1))
     b2[2].direct()
     b2[2].last()
-    raise_rows(1, near(z + 1))
-    b2[1].direct()
-    b2[1].last()
     raise_rows(1, near(z - 1))
     for piece in a2:
         piece.last()
@@ -421,6 +436,7 @@
 
     order = (2, 1, 3, 0)
     sides = (1, -1, 1, -1)
+    net.used = first_x
     ra1 = [
         Scatter(
             net, "tensor", z, d,
@@ -429,6 +445,7 @@
         )
         for i, (j, d) in enumerate(zip(order, sides))
     ]
+    net.used = 0
     rb1 = [
         Scatter(
             net, "batch", y, d,
@@ -437,6 +454,7 @@
         )
         for i, (j, d) in enumerate(zip(order, sides))
     ]
+    net.used = token_pieces[0].n
     minor = [(kk, dc) for kk in range(2) for dc in range(2)]
 
     def strip(kk, dc):
@@ -462,8 +480,9 @@
     lower_rows(0, near(z + 2))
     for piece in ra1:
         piece.send_far()
-    b2[3].direct()
-    b2[3].last()
+    for piece in b2[4:]:
+        piece.direct()
+        piece.last()
     raise_rows(1, near(z + 2), last=True)
     lower_rows(1, near(z + 2))
     rb1[0].send_far()
@@ -560,13 +579,10 @@
     for piece in out_pieces.values():
         piece.last()
 
-    for piece in mix_pieces:
-        piece.direct()
-        piece.last()
     net.drain()
 
 
-MESSAGES = 192
+SENDS, ARRIVALS = 40, 113
 
 
 def local(tokens, gain, phi, w_gate, w_up, w_down):
@@ -604,8 +620,8 @@
         vmem((3, 4, 16, width), BF16),
         vmem((4, 2, 16, width), BF16),
         pltpu.SemaphoreType.DMA((5,)),
-        pltpu.SemaphoreType.DMA((MESSAGES,)),
-        pltpu.SemaphoreType.DMA((MESSAGES,)),
+        pltpu.SemaphoreType.DMA((SENDS,)),
+        pltpu.SemaphoreType.DMA((ARRIVALS,)),
     ]
     anywhere = pl.BlockSpec(memory_space=pltpu.HBM)
     inside = pl.BlockSpec(memory_space=vmem)

time: 103 us -> 101 us (0.981)
  Pallas kernels: 102 us -> 99.3 us
    pallas_call x1, Pallas kernels: 102 us -> 99.3 us  [local(): pl.pallas_call(kernel, out_shape=[jax.ShapeDtypeStruct((RING, rows, slots...]
where the time goes in v5:
time: 101 us
  Pallas kernels  99.3 us (98%)
  matrix products  1.24 us (1%)
    pallas_call x1, Pallas kernels, local(): pl.pallas_call(kernel, out_shape=[jax.ShapeDtypeStruct((RING, rows, slots...  99.3 us

profile of v5, /device:TPU:0, one launch (start us, length us, event | category | flops | bytes accessed | tf_op | source)
XLA Modules:
  0.0 100.5 jit_solution(13130043430219723955)
XLA Ops:
  0.0 99.3 %soft_moe.1 = (bf16[4,64,512]{2,1,0:T(8,128)(2,1)S(1)}, bf16[4,8,16,1024]{3,2,1,0:T(8,128)(2,1)S(1)}) custom-call(bf16[256,1024]{1,0:T(8,128)(2,1)} %bitcast.16, bf16[8,128]{1,0:T(8,128)(2,1)} %bitcast.17, bf16[1024,512]{1,0:T(8,128)(2,1)} %phi_in.1, bf16[4096,896]{1,0:T(8,128)(2,1)} %bitcast.13, bf16[4096,896]{1,0:T(8,128)(2,1)} %bitcast.14, ...), custom_call_target="tpu_custom_call" | custom-call | tf_op jit(solution)/shard_map/soft_moe/pallas_call | solution.py:628
  99.3 1.2 %fusion = bf16[1,256,1024]{2,1,0:T(8,128)(2,1)} fusion(bf16[256,512]{1,0:T(8,128)(2,1)S(1)} %bitcast.12, bf16[512,1024]{1,0:T(8,128)(2,1)S(1)} %bitcast.11), kind=kOutput, calls=%fused_computation.1 | convolution fusion | flops 268697600 | bytes 1835008 | tf_op jit(solution)/shard_map/dot_general | solution.py:642

commit v6 on v5

--- a/solution.py
+++ b/solution.py
@@ -114,7 +114,7 @@
 def kernel(
     tok_in, gain, phi_in, wg_in, wu_in, wd_in, cb, rf,
     tok, phi, wg, wu, wd, tg,
-    lp, l_in, sq_out, sq_in, st, qo, qg, qt,
+    lp, l_in, sq_out, sq_in, sx, st, qo, qg, qt,
     si, xs, acc, hid, ys,
     a_in, a_sum, a2_in, b_in, b_sum, b2_in, so,
     load_sems, send_sems, recv_sems,
@@ -223,10 +223,10 @@
     local_max = jnp.max(logits, axis=0, keepdims=True)
     raised = jnp.exp(logits - local_max)
     local_total = jnp.sum(raised, axis=0, keepdims=True)
-    mine = st.at[y, z]
     for k in range(RING):
-        mine[k : k + 1, :] = local_max[:, k * 128 : (k + 1) * 128]
-        mine[4 + k : 5 + k, :] = local_total[:, k * 128 : (k + 1) * 128]
+        sx[k, 0:1, :] = local_max[:, k * 128 : (k + 1) * 128]
+        sx[k, 1:2, :] = local_total[:, k * 128 : (k + 1) * 128]
+    st[y, z] = sx[y]
     factor = (raised * inv_rms).astype(BF16)
     for k in range(RING):
         qo[k] = factor[:, k * 128 : (k + 1) * 128]
@@ -245,7 +245,7 @@
     spread(0)
     first_st = net.take(len(plane))
     for k, step in enumerate(plane):
-        net.start(first_st + k, mine, mine, in_plane(*step))
+        net.start(first_st + k, sx.at[near(y + step[0])], st.at[y, z], in_plane(*step))
     token_pieces[3].start()
     token_pieces[0].relay()
     token_pieces[1].relay()
@@ -267,8 +267,8 @@
     token_pieces[3].relay()
     for k, (dy, dz) in enumerate(plane):
         net.arrived(first_st + k, st.at[near(y - dy), near(z - dz)], in_plane(dy, dz))
-    maxima = st[:, :, pl.ds(y, 1), :]
-    totals = st[:, :, pl.ds(RING + y, 1), :]
+    maxima = st[:, :, 0:1, :]
+    totals = st[:, :, 1:2, :]
     top = jnp.max(jnp.max(maxima, axis=1, keepdims=True), axis=0, keepdims=True)
     weights = jnp.exp(maxima - top)
     total = jnp.sum(jnp.sum(totals * weights, axis=1, keepdims=True), axis=0, keepdims=True)
@@ -291,7 +291,7 @@
 
     def place(k, core, part):
         inside = pl.ds(k // 2 * 32 + core * 16, 16)
-        return xs.at[z, k % 2, y, inside, pl.ds(part * 2 * tile, 2 * tile)]
+        return xs.at[z, (k + 1) % 2, y, inside, pl.ds(part * 2 * tile, 2 * tile)]
 
     first_x = net.take(2 * len(across))
     for part in range(2):
@@ -347,18 +347,18 @@
     ]
 
     wait_x(0)
+    b1[0].start()
+    b2[0].start()
+    wait_x(1)
     a1[0].start()
     a2[0].start()
-    wait_x(1)
-    b1[0].start()
-    b2[0].start()
     wait_x(3)
+    a1[1].start()
+    wait_x(2)
     b1[1].start()
-    wait_x(2)
-    a1[1].start()
+    a2[1].start()
     b2[1].start()
-    a2[1].start()
-    for piece in (*a1, *b1):
+    for piece in (b1[0], *a1, b1[1]):
         piece.relay()
     for stage, later in ((a1, a2), (b1, b2)):
         for piece in stage:
@@ -516,8 +516,8 @@
         sums[near(me + order[n])] = pieces[n].finish().astype(BF16)
 
     both = (
-        (ra1, a_sum, y, (ra2[2], ra2[0]), (ra2[3], ra2[1])),
-        (rb1, b_sum, z, (rb2[0], rb2[2]), (rb2[1], rb2[3])),
+        (ra1, a_sum, y, (ra2[0], ra2[2]), (ra2[1], ra2[3])),
+        (rb1, b_sum, z, (rb2[2], rb2[0]), (rb2[3], rb2[1])),
     )
     for stage, sums, me, plus, minus in both:
         close_sum(stage, 0, sums, me)
@@ -539,7 +539,7 @@
 
     first_back = net.take(len(across))
     backs = {step: first_back + n for n, step in enumerate(across)}
-    for k, stage in ((1, rb2), (2, ra2), (3, rb2), (0, ra2)):
+    for k, stage in ((2, rb2), (0, rb2), (1, ra2), (3, ra2)):
         for dc in range(2):
             done = stage[k // 2 * 2 + dc].finish().astype(BF16)
             if (k, dc) == (0, 0):
@@ -566,12 +566,12 @@
             out_pieces[k, dc].start()
 
     start_out(0)
+    start_out(2)
     start_out(1)
-    start_out(3)
     for dc in range(2):
         out_pieces[0, dc].relay()
-    start_out(2)
-    for k in (1, 3, 2):
+    start_out(3)
+    for k in (2, 1, 3):
         for dc in range(2):
             out_pieces[k, dc].relay()
     for piece in out_pieces.values():
@@ -603,7 +603,8 @@
         vmem((3, 4, 16, slots), F32),
         vmem((RING, 8, 128), F32),
         vmem((3, 8, 128), F32),
-        vmem((RING, RING, 8, 128), F32),
+        vmem((RING, 2, 128), F32),
+        vmem((RING, RING, 2, 128), F32),
         vmem((RING, rows, 128), BF16),
         vmem((RING, RING, rows, 128), BF16),
         vmem((128, RING * count), BF16),

time: 101 us -> 99.8 us (0.988)
  no operation moved by 1% of the time
where the time goes in v6:
time: 99.8 us; the launch traced here: 99.6 us
  Pallas kernels  98.3 us (98%)
  matrix products  1.24 us (1%)
    pallas_call x1, Pallas kernels, local(): pl.pallas_call(kernel, out_shape=[jax.ShapeDtypeStruct((RING, rows, slots...  98.3 us

profile of v6, /device:TPU:0, one launch (start us, length us, event | category | flops | bytes accessed | tf_op | source)
XLA Modules:
  0.0 99.6 jit_solution(13173336655112099866)
XLA Ops:
  0.0 98.3 %soft_moe.1 = (bf16[4,64,512]{2,1,0:T(8,128)(2,1)S(1)}, bf16[4,8,16,1024]{3,2,1,0:T(8,128)(2,1)S(1)}) custom-call(bf16[256,1024]{1,0:T(8,128)(2,1)} %bitcast.16, bf16[8,128]{1,0:T(8,128)(2,1)} %bitcast.17, bf16[1024,512]{1,0:T(8,128)(2,1)} %phi_in.1, bf16[4096,896]{1,0:T(8,128)(2,1)} %bitcast.13, bf16[4096,896]{1,0:T(8,128)(2,1)} %bitcast.14, ...), custom_call_target="tpu_custom_call" | custom-call | tf_op jit(solution)/shard_map/soft_moe/pallas_call | solution.py:629
  98.3 1.2 %fusion = bf16[1,256,1024]{2,1,0:T(8,128)(2,1)} fusion(bf16[256,512]{1,0:T(8,128)(2,1)S(1)} %bitcast.12, bf16[512,1024]{1,0:T(8,128)(2,1)S(1)} %bitcast.11), kind=kOutput, calls=%fused_computation.1 | convolution fusion | flops 268697600 | bytes 1835008 | tf_op jit(solution)/shard_map/dot_general | solution.py:643

commit v7 on v6

--- a/solution.py
+++ b/solution.py
@@ -502,9 +502,9 @@
     ra1[0].relay()
     ra1[1].relay()
     lower_rows(1, z)
+    rb1[0].relay()
     rb1[3].send_far()
     rb1[3].send_near()
-    rb1[0].relay()
     lower_rows(0, z)
     ra1[2].relay()
     ra1[3].relay()

time: 99.8 us -> 99.8 us (level)
  no operation moved by 1% of the time
where the time goes in v7:
time: 99.8 us; the launch traced here: 99.6 us
  Pallas kernels  98.3 us (98%)
  matrix products  1.24 us (1%)
    pallas_call x1, Pallas kernels, local(): pl.pallas_call(kernel, out_shape=[jax.ShapeDtypeStruct((RING, rows, slots...  98.3 us

profile of v7, /device:TPU:0, one launch (start us, length us, event | category | flops | bytes accessed | tf_op | source)
XLA Modules:
  0.0 99.6 jit_solution(759111147101652928)
XLA Ops:
  0.0 98.3 %soft_moe.1 = (bf16[4,64,512]{2,1,0:T(8,128)(2,1)S(1)}, bf16[4,8,16,1024]{3,2,1,0:T(8,128)(2,1)S(1)}) custom-call(bf16[256,1024]{1,0:T(8,128)(2,1)} %bitcast.16, bf16[8,128]{1,0:T(8,128)(2,1)} %bitcast.17, bf16[1024,512]{1,0:T(8,128)(2,1)} %phi_in.1, bf16[4096,896]{1,0:T(8,128)(2,1)} %bitcast.13, bf16[4096,896]{1,0:T(8,128)(2,1)} %bitcast.14, ...), custom_call_target="tpu_custom_call" | custom-call | tf_op jit(solution)/shard_map/soft_moe/pallas_call | solution.py:629
  98.3 1.2 %fusion = bf16[1,256,1024]{2,1,0:T(8,128)(2,1)} fusion(bf16[256,512]{1,0:T(8,128)(2,1)S(1)} %bitcast.12, bf16[512,1024]{1,0:T(8,128)(2,1)S(1)} %bitcast.11), kind=kOutput, calls=%fused_computation.1 | convolution fusion | flops 268697600 | bytes 1835008 | tf_op jit(solution)/shard_map/dot_general | solution.py:643
